TPU v7x, 256 devices: a whole 4x4x8 slice. The times are simulated.
256 devices in a mesh: blk: 4 (over x), grp: 64 (over z, y, core).
Axes of the slice: x: 4, y: 4, z: 8, core: 2. Of those that a mesh axis runs over, the one named last changes fastest.
Arguments:
- points: float32 [3, 32768], P(None, ('blk', 'grp')), may hold values from 0 to 1
- labels: int32 [32768], P(('blk', 'grp')), may hold values 0 or 1
- shape_scale: float32 [32768], P(('blk', 'grp')), may hold values from 0.1 to 0.4
- krylov_basis: float32 [8, 32, 32768], P(None, None, ('blk', 'grp')), may hold values from -6 to 6
- sketch: float32 [1024, 32768], P(None, ('blk', 'grp')), may hold values from -0.03125 to 0.03125
- sketched_basis: float32 [8, 32, 1024], replicated, may hold values from -0.1875 to 0.1875
Outputs:
- next_vector: float32 [32, 32768], P(None, ('blk', 'grp'))
- coefficients: float32 [8, 32], replicated
- sketch_next: float32 [32, 1024], replicated
- norms: float32 [32], replicated
All inputs are finite; a program needn't handle non-finite values. No bound on the sum of `labels` on one device may be relied on, other than what follows from the above.
Results may differ from a plain program's by a relative error of at most 0.0003.
Values sent between devices are 32-bit elements; how exact they have to be, the bound alone decides.
No kernel may reach another device: no remote copies, remote signals or barrier semaphores. Data moves between devices by JAX's collectives and lax.ppermute only.
A program may use at most 64 MiB of HBM per device.

v0:
```python
import math

import jax
import jax.numpy as jnp
from jax import lax
from jax.sharding import Mesh
from jax.sharding import PartitionSpec as P

SYSTEMS = 32
KRYLOV = 8
GRP = ("grp_0", "grp_1", "grp_2")
BLK_GRP = ("blk", "grp_0", "grp_1", "grp_2")


def copy_for_each(value, axis):
    count = lax.axis_size(axis)
    return lax.all_to_all(
        jnp.broadcast_to(value[None], (count, *value.shape)), axis, 0, 0, tiled=True
    )


def in_order(tiles, dim):
    tiles = jnp.moveaxis(tiles, 0, dim)
    dims = tiles.shape
    return tiles.reshape(*dims[:dim], dims[dim] * dims[dim + 1], *dims[dim + 2 :])


def gather_directly(value, axis, dim):
    tiles = copy_for_each(value, axis)
    return in_order(tiles, dim)


def in_blocks(value, dim, count):
    dims = value.shape
    tiles = value.reshape(*dims[:dim], count, dims[dim] // count, *dims[dim + 1 :])
    return jnp.moveaxis(tiles, dim, 0)


def sum_at_owner(value, axis, dim):
    count = lax.axis_size(axis)
    tiles = lax.all_to_all(in_blocks(value, dim, count), axis, 0, 0, tiled=True)
    return jnp.sum(tiles, axis=0)


def sum_in_two_steps(value, axes, dim):
    far, near = axes
    own = sum_at_owner(in_blocks(value, dim, lax.axis_size(far)), near, dim + 1)
    return jnp.sum(lax.all_to_all(own, far, 0, 0, tiled=True), axis=0)


def padded_to(lines, count):
    spare = -len(lines) % count
    return jnp.pad(lines, [(0, spare)] + [(0, 0)] * (lines.ndim - 1))


def whole_of(value, axes, dim):
    far, near = axes
    leading = copy_for_each(value, far)
    tiles = jnp.swapaxes(copy_for_each(leading, near), 0, 1)
    return in_order(tiles.reshape(-1, *value.shape), dim)


def nested_sum(value, axes):
    lines = value.reshape(-1)
    own = sum_in_two_steps(
        padded_to(lines, lax.axis_size(axes[0]) * lax.axis_size(axes[1])), axes, 0
    )
    whole = whole_of(own, axes, 0)
    return whole[: len(lines)].reshape(value.shape)


def kernel_terms(target_points, target_labels, source_block):
    source_points = source_block[0:3]
    scales = source_block[3]
    weights_block = source_block[4:]
    delta_x = source_points[0][:, None] - target_points[0][None, :]
    delta_y = source_points[1][:, None] - target_points[1][None, :]
    delta_z = source_points[2][:, None] - target_points[2][None, :]
    radius_sq = delta_x * delta_x + delta_y * delta_y + delta_z * delta_z
    squared_scale = (scales * scales)[:, None]
    shifted = radius_sq + squared_scale
    inverse = lax.rsqrt(shifted)
    boundary = shifted * inverse
    interior = (3.0 * squared_scale + 2.0 * radius_sq) * inverse * inverse * inverse
    kernel = jnp.where(target_labels[None, :] == 1, interior, boundary)
    return jnp.dot(
        weights_block, kernel, precision=lax.Precision.HIGHEST, preferred_element_type=jnp.float32
    )


def block_size(length, wanted):
    return wanted if length % wanted == 0 else length


def accumulate(running, target_points, target_labels, source_block):
    target_count = target_points.shape[1]
    source_count = source_block.shape[1]
    tblock = block_size(target_count, 2048)
    sblock = block_size(source_count, 2048)
    system_rows = running.shape[0]

    def over_targets(target_index, current):
        offset = target_index * tblock
        block_points = lax.dynamic_slice_in_dim(target_points, offset, tblock, 1)
        block_labels = lax.dynamic_slice_in_dim(target_labels, offset, tblock, 0)

        def over_sources(source_index, partial_value):
            return partial_value + kernel_terms(block_points, block_labels, source_block)

        partial_value = lax.fori_loop(
            0, source_count // sblock, over_sources, jnp.zeros((system_rows, tblock), jnp.float32)
        )
        previous = lax.dynamic_slice_in_dim(current, offset, tblock, 1)
        return lax.dynamic_update_slice_in_dim(current, previous + partial_value, offset, 1)

    return lax.fori_loop(0, target_count // tblock, over_targets, running)


def shards(points, labels, shape_scale, krylov_basis, sketch, sketched_basis):
    own_count = points.shape[1]
    everything = lax.axis_size("blk") * lax.axis_size(GRP) * own_count
    sources = jnp.concatenate([points, shape_scale[None, :], krylov_basis[KRYLOV - 1]], axis=0)
    quarter_points, quarter_labels = (
        gather_directly(points, GRP, 1),
        gather_directly(labels, GRP, 0),
    )
    empty = jnp.zeros((SYSTEMS, quarter_points.shape[1]), jnp.float32)
    partial_value = accumulate(
        empty, quarter_points, quarter_labels, gather_directly(sources, "blk", 1)
    )
    summed = sum_in_two_steps(partial_value, (("grp_0", "grp_1"), "grp_2"), 1)
    image = summed / math.sqrt(everything)
    local_sketch = lax.dot_general(
        image,
        sketch,
        (((1,), (1,)), ((), ())),
        precision=lax.Precision.HIGHEST,
        preferred_element_type=jnp.float32,
    )
    sketched = nested_sum(local_sketch, (("blk", "grp_0"), ("grp_1", "grp_2")))
    coefficients = jnp.einsum(
        "jrk,rk->jr", sketched_basis, sketched, precision=lax.Precision.HIGHEST
    )
    remainder = sketched - jnp.einsum(
        "jr,jrk->rk", coefficients, sketched_basis, precision=lax.Precision.HIGHEST
    )
    norms = jnp.sqrt(jnp.mean(remainder * remainder, axis=1) + 1e-06)
    sketch_next = remainder / norms[:, None]
    reduced = image - jnp.einsum(
        "jr,jrn->rn", coefficients, krylov_basis, precision=lax.Precision.HIGHEST
    )
    next_vector = reduced / norms[:, None]
    return (next_vector, coefficients, sketch_next, norms)


def solution(mesh):
    torus = Mesh(
        mesh.devices.reshape(mesh.shape["blk"], 8, 4, 2), ("blk", "grp_0", "grp_1", "grp_2")
    )
    in_specs = (
        P(None, BLK_GRP),
        P(BLK_GRP),
        P(BLK_GRP),
        P(None, None, BLK_GRP),
        P(None, BLK_GRP),
        P(),
    )
    out_specs = (P(None, BLK_GRP), P(), P(), P())
    return jax.shard_map(
        shards, mesh=torus, in_specs=in_specs, out_specs=out_specs, check_vma=False
    )
```

profile of v0, /device:TPU:1, one launch (start us, length us, event | category | flops | bytes accessed | tf_op | source)
XLA Modules:
  0.0 151.8 jit_solution(9134515445987639077)
XLA Ops:
  0.6 0.0 copy-start
  0.6 0.8 slice_bitcast_fusion
  1.5 0.7 pad_maximum_fusion
  2.2 9.2 %all_to_all.51 = f32[4,36,128]{2,1,0:T(8,128)S(1)} all-to-all(f32[4,36,128]{2,1,0:T(8,128)S(1)} %broadcast_in_dim.72), channel_id=1, replica_groups=mesh['blk'=4,'grp_0'=8,'grp_1'=4,'grp_2'=2] {'blk'}, dimensions={0} | all-to-all | bytes 147456 | tf_op jit(solution)/shard_map/all_to_all | solution.py:17
  11.4 1.3 broadcast_in_dim.70
  12.7 13.8 %all-to-all-start = ((s32[64,1,128]{2,1,0:T(1,128)}), s32[64,1,128]{2,1,0:T(1,128)S(1)}, u32[]{:S(2)}, u32[]{:S(2)}) async-start(s32[64,1,128]{2,1,0:T(1,128)} %broadcast_in_dim.70), calls=%async_computation | async-start | bytes 65536 | tf_op jit(solution)/shard_map/all_to_all | solution.py:17
  26.5 9.3 %all-to-all-done = s32[64,1,128]{2,1,0:T(1,128)S(1)} async-done(((s32[64,1,128]{2,1,0:T(1,128)}), s32[64,1,128]{2,1,0:T(1,128)S(1)}, u32[]{:S(2)}, u32[]{:S(2)}) %all-to-all-start) | async-done | bytes 32800 | tf_op jit(solution)/shard_map/all_to_all | solution.py:17
  35.7 1.4 broadcast_in_dim.73
  37.1 4.7 %all-to-all-start.2 = ((f32[64,3,128]{2,1,0:T(4,128)}), f32[64,3,128]{2,1,0:T(4,128)S(1)}, u32[]{:S(2)}, u32[]{:S(2)}) async-start(f32[64,3,128]{2,1,0:T(4,128)} %broadcast_in_dim.73), calls=%async_computation.2 | async-start | bytes 262144 | tf_op jit(solution)/shard_map/all_to_all | solution.py:17
  41.9 11.3 %all-to-all-done.2 = f32[64,3,128]{2,1,0:T(4,128)S(1)} async-done(((f32[64,3,128]{2,1,0:T(4,128)}), f32[64,3,128]{2,1,0:T(4,128)S(1)}, u32[]{:S(2)}, u32[]{:S(2)}) %all-to-all-start.2) | async-done | bytes 98336 | tf_op jit(solution)/shard_map/all_to_all | solution.py:17
  53.2 0.1 broadcast_in_dim.69
  53.2 20.0 %while.23 = (s32[]{:T(128)}, f32[32,8192]{1,0:T(8,128)S(1)}, s32[8192]{0:T(1024)S(1)}, f32[512,1]{0,1:T(1,128)S(1)}, f32[36,512]{1,0:T(8,128)S(1)}, /*index=5*/f...) while((s32[]{:T(128)}, f32[32,8192]{1,0:T(8,128)S(1)}, ...), condition=%wide.region_1.0_spmd, body=%wide.region_0.1_spmd.sunk | while | flops 419498496 | bytes 702671 | solution.py:116
  53.3 0.1 constant_dynamic-slice_fusion.2
  53.4 4.8 %fusion.59 = f32[32,8192]{1,0:T(8,128)S(1)} fusion(f32[32,8192]{1,0:T(8,128)S(1)} %get-tuple-element.245, s32[]{:T(128)S(6)} %select_n.34, f32[512]{0:T(512)S(1)} %bitcast.106, f32[2048]{0:T(1024)S(1)} %bitcast.102, f32[512]{0:T(512)S(1)} %bitcast.111, f32[2048]{0:T(1024)S(1)} %bitcast.101, f32[512]{0:T(512)S(1)} %bitcast.112, ...), kind=kOutput, calls=%fused_computation.17.clone.1 | convolution fusion | flops 419495936 | bytes 626692 | tf_op jit(solution)/shard_map/while/body/eval_jaxpr/while/body/eval_jaxpr/dot_general | solution.py:86
  58.3 0.1 constant_dynamic-slice_fusion.2
  58.4 4.8 %fusion.59 = f32[32,8192]{1,0:T(8,128)S(1)} fusion(f32[32,8192]{1,0:T(8,128)S(1)} %get-tuple-element.245, s32[]{:T(128)S(6)} %select_n.34, f32[512]{0:T(512)S(1)} %bitcast.106, f32[2048]{0:T(1024)S(1)} %bitcast.102, f32[512]{0:T(512)S(1)} %bitcast.111, f32[2048]{0:T(1024)S(1)} %bitcast.101, f32[512]{0:T(512)S(1)} %bitcast.112, ...), kind=kOutput, calls=%fused_computation.17.clone.1 | convolution fusion | flops 419495936 | bytes 626692 | tf_op jit(solution)/shard_map/while/body/eval_jaxpr/while/body/eval_jaxpr/dot_general | solution.py:86
  63.3 0.1 constant_dynamic-slice_fusion.2
  63.4 4.8 %fusion.59 = f32[32,8192]{1,0:T(8,128)S(1)} fusion(f32[32,8192]{1,0:T(8,128)S(1)} %get-tuple-element.245, s32[]{:T(128)S(6)} %select_n.34, f32[512]{0:T(512)S(1)} %bitcast.106, f32[2048]{0:T(1024)S(1)} %bitcast.102, f32[512]{0:T(512)S(1)} %bitcast.111, f32[2048]{0:T(1024)S(1)} %bitcast.101, f32[512]{0:T(512)S(1)} %bitcast.112, ...), kind=kOutput, calls=%fused_computation.17.clone.1 | convolution fusion | flops 419495936 | bytes 626692 | tf_op jit(solution)/shard_map/while/body/eval_jaxpr/while/body/eval_jaxpr/dot_general | solution.py:86
  68.3 0.1 constant_dynamic-slice_fusion.2
  68.4 4.8 %fusion.59 = f32[32,8192]{1,0:T(8,128)S(1)} fusion(f32[32,8192]{1,0:T(8,128)S(1)} %get-tuple-element.245, s32[]{:T(128)S(6)} %select_n.34, f32[512]{0:T(512)S(1)} %bitcast.106, f32[2048]{0:T(1024)S(1)} %bitcast.102, f32[512]{0:T(512)S(1)} %bitcast.111, f32[2048]{0:T(1024)S(1)} %bitcast.101, f32[512]{0:T(512)S(1)} %bitcast.112, ...), kind=kOutput, calls=%fused_computation.17.clone.1 | convolution fusion | flops 419495936 | bytes 626692 | tf_op jit(solution)/shard_map/while/body/eval_jaxpr/while/body/eval_jaxpr/dot_general | solution.py:86
  73.3 0.1 copy.55
  73.4 0.5 reshape.85
  74.0 0.6 copy.20
  74.6 4.6 %all_to_all.52 = f32[2,32,32,128]{3,1,2,0:T(8,128)S(1)} all-to-all(f32[2,32,32,128]{3,1,2,0:T(8,128)S(1)} %copy.20), channel_id=1, replica_groups=mesh['blk'=4,'grp_0'=8,'grp_1'=4,'grp_2'=2] {'grp_2'}, dimensions={0} | all-to-all | bytes 2097152 | tf_op jit(solution)/shard_map/all_to_all | solution.py:41
  79.2 0.1 reduce_sum.45
  79.3 0.3 copy.22
  79.6 0.0 copy-start.1
  79.6 19.7 %all_to_all.53 = f32[32,32,128]{2,1,0:T(8,128)S(1)} all-to-all(f32[32,32,128]{2,1,0:T(8,128)S(1)} %copy.22), channel_id=1, replica_groups=mesh['blk'=4,'grp_0'=8,'grp_1'=4,'grp_2'=2] {'grp_0','grp_1'}, dimensions={0} | all-to-all | bytes 1048576 | tf_op jit(solution)/shard_map/all_to_all | solution.py:48
  99.4 0.0 copy-done.1
  99.4 0.6 convolution_bitcast_fusion
  100.0 10.8 %all_to_all.54 = f32[8,32,128]{2,1,0:T(8,128)S(1)} all-to-all(f32[8,32,128]{2,1,0:T(8,128)S(1)} %bitcast.95), channel_id=1, replica_groups=mesh['blk'=4,'grp_0'=8,'grp_1'=4,'grp_2'=2] {'grp_1','grp_2'}, dimensions={0} | all-to-all | bytes 262144 | tf_op jit(solution)/shard_map/all_to_all | solution.py:41
  110.8 0.0 copy-start.2
  110.8 11.8 %all_to_all.55 = f32[32,1,128]{2,1,0:T(1,128)S(1)} all-to-all(f32[32,1,128]{2,1,0:T(1,128)S(1)} %bitcast.108), channel_id=1, replica_groups=mesh['blk'=4,'grp_0'=8,'grp_1'=4,'grp_2'=2] {'blk','grp_0'}, dimensions={0} | all-to-all | bytes 32768 | tf_op jit(solution)/shard_map/all_to_all | solution.py:48
  122.6 0.1 reduce_sum.48
  122.6 11.6 %all_to_all.56 = f32[32,1,128]{2,1,0:T(1,128)S(1)} all-to-all(f32[32,1,128]{2,1,0:T(1,128)S(1)} %broadcast_in_dim.74), channel_id=1, replica_groups=mesh['blk'=4,'grp_0'=8,'grp_1'=4,'grp_2'=2] {'blk','grp_0'}, dimensions={0} | all-to-all | bytes 32768 | tf_op jit(solution)/shard_map/all_to_all | solution.py:17
  134.3 11.1 %all_to_all.57 = f32[8,32,128]{2,1,0:T(8,128)S(1)} all-to-all(f32[8,32,128]{2,1,0:T(8,128)S(1)} %broadcast_in_dim.76), channel_id=1, replica_groups=mesh['blk'=4,'grp_0'=8,'grp_1'=4,'grp_2'=2] {'grp_1','grp_2'}, dimensions={0} | all-to-all | bytes 262144 | tf_op jit(solution)/shard_map/all_to_all | solution.py:17
  145.3 0.1 copy.24
  145.4 0.0 copy-done
  145.4 2.7 %fusion.37 = f32[32,1,8]{2,1,0:T(1,128)S(1)} fusion(f32[32,1024,1]{1,2,0:T(1,128)S(1)} %bitcast.94, f32[8,32,1024]{2,1,0:T(8,128)S(1)} %copy-done), kind=kOutput, calls=%fused_computation.37 | convolution fusion | flops 3145728 | bytes 1180672 | tf_op jit(solution)/shard_map/jrk,rk->jr/dot_general | solution.py:141
  148.1 0.1 copy.27
  148.2 0.0 copy-start.3
  148.2 0.1 copy.28
  148.3 0.0 copy-done.2
  148.3 0.4 fusion.39
  148.7 1.5 fusion.35
  150.2 0.1 multiply_reduce_fusion
  150.4 0.0 copy-start.4
  150.4 0.7 subtract_divide_fusion
  151.1 0.7 broadcast_divide_fusion
  151.8 0.0 copy-done.3
  151.8 0.0 copy-done.4
  (23 shorter events, 0.3 us)
Async XLA Ops:
  0.6 144.8 %copy-start = (f32[8,32,1024]{2,1,0:T(8,128)S(1)}, f32[8,32,1024]{2,1,0:T(8,128)}, u32[]{:S(2)}) copy-start(f32[8,32,1024]{2,1,0:T(8,128)} %param.13) | copy-start | bytes 3145732
  12.7 23.1 %all-to-all-start = ((s32[64,1,128]{2,1,0:T(1,128)}), s32[64,1,128]{2,1,0:T(1,128)S(1)}, u32[]{:S(2)}, u32[]{:S(2)}) async-start(s32[64,1,128]{2,1,0:T(1,128)} %broadcast_in_dim.70), calls=%async_computation | async-start | bytes 65536 | tf_op jit(solution)/shard_map/all_to_all | solution.py:17
  37.1 16.1 %all-to-all-start.2 = ((f32[64,3,128]{2,1,0:T(4,128)}), f32[64,3,128]{2,1,0:T(4,128)S(1)}, u32[]{:S(2)}, u32[]{:S(2)}) async-start(f32[64,3,128]{2,1,0:T(4,128)} %broadcast_in_dim.73), calls=%async_computation.2 | async-start | bytes 262144 | tf_op jit(solution)/shard_map/all_to_all | solution.py:17
  79.6 19.8 %copy-start.1 = (f32[1024,128]{1,0:T(8,128)S(1)}, f32[1024,128]{1,0:T(8,128)}, u32[]{:S(2)}) copy-start(f32[1024,128]{1,0:T(8,128)} %param.12) | copy-start | bytes 1572868
  110.8 37.5 %copy-start.2 = (f32[8,32,128]{2,1,0:T(8,128)S(1)}, f32[8,32,128]{2,1,0:T(8,128)}, u32[]{:S(2)}) copy-start(f32[8,32,128]{2,1,0:T(8,128)} %param.11) | copy-start | bytes 393220
  148.2 3.6 %copy-start.3 = (f32[32,1,8]{0,2,1:T(8,128)}, f32[32,1,8]{0,2,1:T(8,128)S(1)}, u32[]{:S(2)}) copy-start(f32[32,1,8]{0,2,1:T(8,128)S(1)} %copy.27) | copy-start | bytes 3076
  150.4 1.4 copy-start.4
where the time goes:
time: 152 us
  blocking collectives  78.7 us (52%)
  matrix products  24.5 us (16%)
  waiting for transfers between devices  20.6 us (14%)
  starting transfers between devices  18.5 us (12%)
  local copies, waits for them, and re-layouts  5.89 us (4%)
  other arithmetic  2.57 us (2%)
    all_to_all x3, blocking collectives, copy_for_each(): lax.all_to_all(jnp.broadcast_to(value[None], (count, *value.shape)), axis...  31.9 us
    all_to_all x2, blocking collectives, sum_in_two_steps(): return jnp.sum(lax.all_to_all(own, far, 0, 0, tiled=True), axis=0)  31.5 us
    all_to_all x2, waiting for transfers between devices, copy_for_each(): lax.all_to_all(jnp.broadcast_to(value[None], (count, *value.shape)), axis...  20.6 us
    dot_general x4, matrix products, kernel_terms(): jnp.dot(weights_block, kernel, precision=lax.Precision.HIGHEST, preferred...  19.3 us
    all_to_all x2, starting transfers between devices, copy_for_each(): lax.all_to_all(jnp.broadcast_to(value[None], (count, *value.shape)), axis...  18.5 us
    all_to_all x2, blocking collectives, sum_at_owner(): tiles = lax.all_to_all(in_blocks(value, dim, count), axis, 0, 0, tiled=True)  15.3 us
  transfers between devices with their start and end apart: 2, of which 2 were waited for; matrix products, arithmetic and copies ran while one was open for 0% of the time, Pallas kernels for 0%

commit v1 on v0

v1 whole, which is shorter than its diff:
```python
import functools
import math

import jax
import jax.numpy as jnp
from jax import lax
from jax.experimental import pallas as pl
from jax.experimental.pallas import tpu as pltpu
from jax.sharding import Mesh
from jax.sharding import PartitionSpec as P

SYSTEMS = 32
KRYLOV = 8
FEATS = 32
LANES = 128
ALL = ("blk", "grp_0", "grp_1", "grp_2")
ROW = ("blk", "grp_1")
COLUMN = ("grp_0", "grp_2")
OWNERS = ("blk", "grp_1", "grp_2")
VMEM = pl.BlockSpec(memory_space=pltpu.VMEM)
MIB = 2**20


def exchange(value, axis):
    return lax.all_to_all(value, axis, 0, 0, tiled=True)


def copies(value, axis):
    return jnp.broadcast_to(value[None], (lax.axis_size(axis), *value.shape))


def parts(value):
    first = value.astype(jnp.bfloat16).astype(jnp.float32)
    rest = value - first
    second = rest.astype(jnp.bfloat16).astype(jnp.float32)
    return [first, second, rest - second]


def wide(tiles):
    return jnp.concatenate(tiles, axis=1)


def pair_kernel(tblock, sblock, source_ref, target_ref, out_ref, source_feats, target_feats, squares, weights):
    blocks, owners = source_ref.shape[0], target_ref.shape[0]
    zero = jnp.zeros((blocks, LANES), jnp.float32)
    one = zero + 1.0
    coords = [source_ref[:, SYSTEMS + a, :] - 0.5 for a in range(3)]
    scale = source_ref[:, SYSTEMS + 3, :]
    scale_sq = scale * scale
    rows = []
    for value in coords:
        a, b, c = parts(value)
        rows += [a, a, b, b, a, c]
    rows += parts(coords[0] * coords[0] + coords[1] * coords[1] + coords[2] * coords[2] + scale_sq)
    rows += [one] * 3 + parts(scale_sq)
    rows += [zero] * (FEATS - len(rows))
    for k, value in enumerate(rows):
        source_feats[:, k, :] = value
    zero = jnp.zeros((owners, LANES), jnp.float32)
    one = zero + 1.0
    coords = [target_ref[:, a, :] - 0.5 for a in range(3)]
    rows = []
    for value in coords:
        a, b, c = parts(-2.0 * value)
        rows += [a, b, a, b, c, a]
    rows += [one] * 3
    rows += parts(coords[0] * coords[0] + coords[1] * coords[1] + coords[2] * coords[2])
    rows += [zero] * (FEATS - len(rows))
    for k, value in enumerate(rows):
        target_feats[:, k, :] = value
    row = lax.broadcasted_iota(jnp.int32, (FEATS, LANES), 0)
    pick = jnp.where(jnp.logical_and(row >= 24, row < 27), 1.0, 0.0).astype(jnp.bfloat16)
    steps, per, tper = blocks * LANES // sblock, sblock // LANES, tblock // LANES
    over_rows = (((0,), (0,)), ((), ()))

    def feats_of(step):
        return wide([source_feats[step * per + j] for j in range(per)]).astype(jnp.bfloat16)

    for step in range(steps):
        squares[step * sblock : (step + 1) * sblock, :] = lax.dot_general(
            feats_of(step), pick, over_rows, preferred_element_type=jnp.float32
        )
        weight = wide([source_ref[step * per + j, 0:SYSTEMS, :] for j in range(per)])
        first = weight.astype(jnp.bfloat16)
        second = (weight - first.astype(jnp.float32)).astype(jnp.bfloat16)
        weights[step] = jnp.concatenate([first, second], axis=0)

    def over_targets(index, carry):
        feats = wide([target_feats[index * tper + j] for j in range(tper)]).astype(jnp.bfloat16)
        inner = wide([target_ref[index * tper + j, 3:4, :] for j in range(tper)]) > 0.5
        total = jnp.zeros((2 * SYSTEMS, tblock), jnp.float32)
        for step in range(steps):
            shifted = lax.dot_general(
                feats_of(step), feats, over_rows, preferred_element_type=jnp.float32
            )
            inverse = lax.rsqrt(shifted)
            square = wide([squares[step * sblock : (step + 1) * sblock, :]] * tper)
            kernel = inverse * jnp.where(inner, 2.0 + square * (inverse * inverse), shifted)
            first = kernel.astype(jnp.bfloat16)
            second = (kernel - first.astype(jnp.float32)).astype(jnp.bfloat16)
            weight = weights[step]
            total = (
                total
                + jnp.dot(weight, first, preferred_element_type=jnp.float32)
                + jnp.dot(weight, second, preferred_element_type=jnp.float32)
            )
        result = total[:SYSTEMS] + total[SYSTEMS:]
        for j in range(tper):
            out_ref[index * tper + j] = result[:, j * LANES : (j + 1) * LANES]
        return carry

    lax.fori_loop(0, owners // tper, over_targets, 0)


def pair_product(sources, targets, tblock=256, sblock=128):
    blocks, owners = sources.shape[0], targets.shape[0]
    pairs = blocks * owners * LANES * LANES
    return pl.pallas_call(
        functools.partial(pair_kernel, tblock, sblock),
        out_shape=jax.ShapeDtypeStruct((owners, SYSTEMS, LANES), jnp.float32),
        in_specs=[VMEM] * 2,
        out_specs=VMEM,
        scratch_shapes=[
            pltpu.VMEM((blocks, FEATS, LANES), jnp.float32),
            pltpu.VMEM((owners, FEATS, LANES), jnp.float32),
            pltpu.VMEM((blocks * LANES, LANES), jnp.float32),
            pltpu.VMEM((blocks * LANES // sblock, 2 * SYSTEMS, sblock), jnp.bfloat16),
        ],
        cost_estimate=pl.CostEstimate(flops=6 * SYSTEMS * pairs, bytes_accessed=2**20, transcendentals=pairs),
        name="pairs",
        compiler_params=pltpu.CompilerParams(vmem_limit_bytes=16 * MIB),
    )(sources, targets)


def image_kernel(root, arrived_ref, sketch_ref, image_ref, local_ref):
    total = arrived_ref[0]
    for k in range(1, arrived_ref.shape[0]):
        total = total + arrived_ref[k]
    image = total / root
    image_ref[...] = image
    for k in range(sketch_ref.shape[0] // LANES):
        local_ref[:, k, :] = lax.dot_general(
            image,
            sketch_ref[k * LANES : (k + 1) * LANES, :],
            (((1,), (1,)), ((), ())),
            precision=lax.Precision.HIGHEST,
            preferred_element_type=jnp.float32,
        )


def image_and_sketch(arrived, sketch, root):
    rows = sketch.shape[0]
    return pl.pallas_call(
        functools.partial(image_kernel, root),
        out_shape=(
            jax.ShapeDtypeStruct((SYSTEMS, LANES), jnp.float32),
            jax.ShapeDtypeStruct((SYSTEMS, rows // LANES, LANES), jnp.float32),
        ),
        in_specs=[VMEM] * 2,
        out_specs=(VMEM,) * 2,
        name="image",
        compiler_params=pltpu.CompilerParams(vmem_limit_bytes=8 * MIB),
    )(arrived, sketch)


def sum_kernel(arrived_ref, out_ref):
    total = arrived_ref[0]
    for k in range(1, arrived_ref.shape[0]):
        total = total + arrived_ref[k]
    for k in range(out_ref.shape[0]):
        out_ref[k] = total


def sum_for_each(arrived, count):
    return pl.pallas_call(
        sum_kernel,
        out_shape=jax.ShapeDtypeStruct((count, *arrived.shape[1:]), jnp.float32),
        in_specs=[VMEM],
        out_specs=VMEM,
        name="addup",
        compiler_params=pltpu.CompilerParams(vmem_limit_bytes=4 * MIB),
    )(arrived)


def project_kernel(arrived_ref, basis_ref, out_ref):
    sketched = arrived_ref[0]
    for k in range(1, arrived_ref.shape[0]):
        sketched = sketched + arrived_ref[k]
    lane = lax.broadcasted_iota(jnp.int32, (8, LANES), 1)

    def whole(value):
        return jnp.sum(jnp.sum(value, axis=1, keepdims=True), axis=0, keepdims=True)

    scalars = jnp.zeros((8, LANES), jnp.float32)
    remainder = sketched
    for j in range(KRYLOV):
        coefficient = whole(basis_ref[j] * sketched)
        scalars = jnp.where(lane == j, coefficient, scalars)
        remainder = remainder - coefficient * basis_ref[j]
    norm = jnp.sqrt(whole(remainder * remainder) / (sketched.shape[0] * LANES) + 1e-06)
    scalars = jnp.where(lane == KRYLOV, norm, scalars)
    message = jnp.concatenate([remainder / norm, scalars], axis=0)
    for k in range(out_ref.shape[0]):
        out_ref[k] = message


def project(arrived, basis, count):
    return pl.pallas_call(
        project_kernel,
        out_shape=jax.ShapeDtypeStruct((count, arrived.shape[1] + 8, LANES), jnp.float32),
        in_specs=[VMEM] * 2,
        out_specs=VMEM,
        name="project",
        compiler_params=pltpu.CompilerParams(vmem_limit_bytes=4 * MIB),
    )(arrived, basis)


def finish_kernel(arrived_ref, image_ref, krylov_ref, next_ref, coefficients_ref, sketch_ref, norms_ref):
    rows = arrived_ref.shape[1] - 8
    for k in range(rows):
        sketch_ref[:, k * LANES : (k + 1) * LANES] = arrived_ref[:, k, :]
    scalars = arrived_ref[:, rows, :]
    reduced = image_ref[...]
    for j in range(KRYLOV):
        reduced = reduced - scalars[:, j : j + 1] * krylov_ref[j]
    next_ref[...] = reduced / scalars[:, KRYLOV : KRYLOV + 1]
    across = jnp.transpose(scalars)
    coefficients_ref[...] = across[0:KRYLOV, :]
    norms_ref[...] = across[KRYLOV : KRYLOV + 1, :]


def finish(arrived, image, krylov):
    rows = arrived.shape[1] - 8
    return pl.pallas_call(
        finish_kernel,
        out_shape=(
            jax.ShapeDtypeStruct((SYSTEMS, LANES), jnp.float32),
            jax.ShapeDtypeStruct((KRYLOV, SYSTEMS), jnp.float32),
            jax.ShapeDtypeStruct((SYSTEMS, rows * LANES), jnp.float32),
            jax.ShapeDtypeStruct((1, SYSTEMS), jnp.float32),
        ),
        in_specs=[VMEM] * 3,
        out_specs=(VMEM,) * 4,
        name="finish",
        compiler_params=pltpu.CompilerParams(vmem_limit_bytes=8 * MIB),
    )(arrived, image, krylov)


def shards(points, labels, shape_scale, krylov_basis, sketch, sketched_basis):
    everything = lax.axis_size(ALL) * points.shape[1]
    sources = jnp.concatenate([krylov_basis[KRYLOV - 1], points, shape_scale[None, :]], axis=0)
    targets = jnp.concatenate([points, labels[None, :].astype(jnp.float32)], axis=0)
    system = lax.axis_index(OWNERS)
    basis = lax.dynamic_slice_in_dim(sketched_basis, system, 1, axis=1)
    basis = basis.reshape(KRYLOV, -1, LANES)
    all_targets = exchange(copies(targets, COLUMN), COLUMN)
    all_sources = exchange(copies(sources, ROW), ROW)
    partial_value = pair_product(all_sources, all_targets)
    image, local_sketch = image_and_sketch(
        exchange(partial_value, COLUMN), sketch, math.sqrt(everything)
    )
    over_owners = sum_for_each(exchange(local_sketch, OWNERS), lax.axis_size("grp_0"))
    message = project(exchange(over_owners, "grp_0"), basis, lax.axis_size(OWNERS))
    next_vector, coefficients, sketch_next, norms = finish(
        exchange(message, OWNERS), image, krylov_basis
    )
    return (next_vector, coefficients, sketch_next, norms.reshape(-1))


def solution(mesh):
    torus = Mesh(mesh.devices.reshape(mesh.shape["blk"], 8, 4, 2), ALL)
    in_specs = (P(None, ALL), P(ALL), P(ALL), P(None, None, ALL), P(None, ALL), P())
    out_specs = (P(None, ALL), P(), P(), P())
    return jax.shard_map(
        shards, mesh=torus, in_specs=in_specs, out_specs=out_specs, check_vma=False
    )
```

time: 152 us -> 99 us (0.65)
  blocking collectives: 78.7 us -> 44.8 us
  matrix products: 24.5 us -> 0 us
  Pallas kernels: 0 us -> 11.9 us
  local copies, waits for them, and re-layouts: 5.89 us -> 2.08 us
    all_to_all x7 -> x3, blocking collectives: 78.7 us -> 44.8 us  [exchange(): return lax.all_to_all(value, axis, 0, 0, tiled=True)]
    dot_general x8 -> x0, matrix products: 24.5 us -> none  [the longest x4 19.3 us: kernel_terms(): jnp.dot(weights_block, kernel, precision=lax.Precision.HIGHEST, preferred...]
    pallas_call x0 -> x5, Pallas kernels: none -> 11.9 us  [the longest x1 8.34 us: pair_product(): pl.pallas_call(functools.partial(pair_kernel, tblock, sblock), out_shape=...]
    broadcast_in_dim x6 -> x2, local copies, waits for them, and re-layouts: 2.74 us -> 0.64 us  [copies(): return jnp.broadcast_to(value[None], (lax.axis_size(axis), *value.shape))]
    all_to_all x2 -> x3, starting transfers between devices: 18.5 us -> 17.1 us  [exchange(): return lax.all_to_all(value, axis, 0, 0, tiled=True)]
    all_to_all x2 -> x3, waiting for transfers between devices: 20.6 us -> 20.4 us  [exchange(): return lax.all_to_all(value, axis, 0, 0, tiled=True)]
  transfers between devices with their start and end apart: 2 -> 3, of which waited for: 2 -> 3; matrix products, arithmetic and copies ran while one was open for 0% -> 1% of each run, Pallas kernels for 0% -> 0%
where the time goes in v1:
time: 99 us; the launch traced here: 98.4 us
  blocking collectives  44.8 us (45%)
  waiting for transfers between devices  20.4 us (21%)
  starting transfers between devices  17.1 us (17%)
  Pallas kernels  11.9 us (12%)
  local copies, waits for them, and re-layouts  2.08 us (2%)
  other arithmetic  1.44 us (1%)
    all_to_all x3, blocking collectives, exchange(): return lax.all_to_all(value, axis, 0, 0, tiled=True)  44.8 us
    all_to_all x3, waiting for transfers between devices, exchange(): return lax.all_to_all(value, axis, 0, 0, tiled=True)  20.4 us
    all_to_all x3, starting transfers between devices, exchange(): return lax.all_to_all(value, axis, 0, 0, tiled=True)  17.1 us
    pallas_call x1, Pallas kernels, pair_product(): pl.pallas_call(functools.partial(pair_kernel, tblock, sblock), out_shape=...  8.34 us
  transfers between devices with their start and end apart: 3, of which 3 were waited for; matrix products, arithmetic and copies ran while one was open for 1% of the time, Pallas kernels for 0%

profile of v1, /device:TPU:1, one launch (start us, length us, event | category | flops | bytes accessed | tf_op | source)
XLA Modules:
  0.0 98.4 jit_solution(7250597622474528781)
XLA Ops:
  0.6 0.0 copy-start
  0.6 0.7 convert_bitcast_fusion
  1.4 0.7 pad_maximum_fusion.1
  2.1 0.6 broadcast_in_dim.8
  2.7 10.0 %all-to-all-start.1 = ((f32[16,4,128]{2,1,0:T(4,128)}), f32[16,4,128]{2,1,0:T(4,128)S(1)}, u32[]{:S(2)}, u32[]{:S(2)}) async-start(f32[16,4,128]{2,1,0:T(4,128)} %broadcast_in_dim.8), calls=%async_computation.1 | async-start | bytes 65536 | tf_op jit(solution)/shard_map/all_to_all | solution.py:25
  12.7 0.0 copy-start.3
  12.7 0.7 slice_bitcast_fusion
  13.4 0.0 copy-start.4
  13.4 0.0 copy-done.3
  13.4 0.7 copy-done.4
  14.1 6.0 %all-to-all-done.1.target_ref = f32[16,4,128]{2,1,0:T(4,128)S(1)} async-done(((f32[16,4,128]{2,1,0:T(4,128)}), f32[16,4,128]{2,1,0:T(4,128)S(1)}, u32[]{:S(2)}, u32[]{:S(2)}) %all-to-all-start.1) | async-done | bytes 32800 | tf_op jit(solution)/shard_map/all_to_all | solution.py:25
  20.1 14.5 %all_to_all.30.source_ref = f32[16,36,128]{2,1,0:T(8,128)S(1)} all-to-all(f32[16,36,128]{2,1,0:T(8,128)S(1)} %broadcast_in_dim.7), channel_id=1, replica_groups=mesh['blk'=4,'grp_0'=8,'grp_1'=4,'grp_2'=2] {'blk','grp_1'}, dimensions={0} | all-to-all | bytes 589824 | tf_op jit(solution)/shard_map/all_to_all | solution.py:25
  34.6 8.3 %pairs.1 = f32[16,32,128]{2,1,0:T(8,128)S(1)} custom-call(f32[16,36,128]{2,1,0:T(8,128)S(1)} %all_to_all.30.source_ref, f32[16,4,128]{2,1,0:T(4,128)S(1)} %all-to-all-done.1.target_ref), custom_call_target="tpu_custom_call" | custom-call | flops 805306368 | bytes 1048576 | tf_op jit(solution)/shard_map/pairs/pallas_call | solution.py:118
  42.9 0.0 copy-start.1
  42.9 16.5 %all_to_all.31.arrived_ref = f32[16,32,128]{2,1,0:T(8,128)S(1)} all-to-all(f32[16,32,128]{2,1,0:T(8,128)S(1)} %pairs.1), channel_id=1, replica_groups=mesh['blk'=4,'grp_0'=8,'grp_1'=4,'grp_2'=2] {'grp_0','grp_2'}, dimensions={0} | all-to-all | bytes 524288 | tf_op jit(solution)/shard_map/all_to_all | solution.py:25
  59.4 0.0 copy-done.1
  59.4 1.6 %image.1 = (f32[32,128]{1,0:T(8,128)S(1)}, f32[32,8,128]{2,1,0:T(8,128)}) custom-call(f32[16,32,128]{2,1,0:T(8,128)S(1)} %all_to_all.31.arrived_ref, f32[1024,128]{1,0:T(8,128)S(1)} %copy-done.1), custom_call_target="tpu_custom_call" | custom-call | tf_op jit(solution)/shard_map/image/pallas_call | solution.py:153
  61.0 3.8 %all-to-all-start.3 = ((f32[32,8,128]{2,1,0:T(8,128)}), f32[32,8,128]{2,1,0:T(8,128)S(1)}, u32[]{:S(2)}, u32[]{:S(2)}) async-start(f32[32,8,128]{2,1,0:T(8,128)} %get-tuple-element.10), calls=%async_computation.3 | async-start | bytes 262144 | tf_op jit(solution)/shard_map/all_to_all | solution.py:25
  64.9 7.7 %all-to-all-done.3.arrived_ref = f32[32,8,128]{2,1,0:T(8,128)S(1)} async-done(((f32[32,8,128]{2,1,0:T(8,128)}), f32[32,8,128]{2,1,0:T(8,128)S(1)}, u32[]{:S(2)}, u32[]{:S(2)}) %all-to-all-start.3) | async-done | bytes 131104 | tf_op jit(solution)/shard_map/all_to_all | solution.py:25
  72.5 0.6 addup.1
  73.2 3.3 %all-to-all-start.4 = ((f32[8,8,128]{2,1,0:T(8,128)}), f32[8,8,128]{2,1,0:T(8,128)S(1)}, u32[]{:S(2)}, u32[]{:S(2)}) async-start(f32[8,8,128]{2,1,0:T(8,128)} %addup.1), calls=%async_computation.4 | async-start | bytes 65536 | tf_op jit(solution)/shard_map/all_to_all | solution.py:25
  76.5 0.0 copy-done
  76.6 6.7 %all-to-all-done.4.arrived_ref = f32[8,8,128]{2,1,0:T(8,128)S(1)} async-done(((f32[8,8,128]{2,1,0:T(8,128)}), f32[8,8,128]{2,1,0:T(8,128)S(1)}, u32[]{:S(2)}, u32[]{:S(2)}) %all-to-all-start.4) | async-done | bytes 32800 | tf_op jit(solution)/shard_map/all_to_all | solution.py:25
  83.3 0.2 project.1
  83.6 0.0 copy-start.2
  83.6 13.8 %all_to_all.32.arrived_ref = f32[32,16,128]{2,1,0:T(8,128)S(1)} all-to-all(f32[32,16,128]{2,1,0:T(8,128)S(1)} %project.1), channel_id=1, replica_groups=mesh['blk'=4,'grp_0'=8,'grp_1'=4,'grp_2'=2] {'blk','grp_1','grp_2'}, dimensions={0} | all-to-all | bytes 524288 | tf_op jit(solution)/shard_map/all_to_all | solution.py:25
  97.4 0.0 copy-done.2
  97.4 1.1 %finish.1 = (f32[32,128]{1,0:T(8,128)}, f32[8,32]{1,0:T(8,128)}, f32[32,1024]{1,0:T(8,128)}, f32[1,32]{1,0:T(1,128)}) custom-call(f32[32,16,128]{2,1,0:T(8,128)S(1)} %all_to_all.32.arrived_ref, f32[32,128]{1,0:T(8,128)S(1)} %get-tuple-element.11.image_ref, f32[8,32,128]{2,1,0:T(8,128)S(1)} %copy-done.2), custom_call_target="tpu_custom_call" | custom-call | tf_op jit(solution)/shard_map/finish/pallas_call | solution.py:234
  (3 shorter events, 0.1 us)
Async XLA Ops:
  0.6 75.9 %copy-start = (f32[8,32,1024]{2,1,0:T(8,128)S(1)}, f32[8,32,1024]{2,1,0:T(8,128)}, u32[]{:S(2)}) copy-start(f32[8,32,1024]{2,1,0:T(8,128)} %param.11) | copy-start | bytes 3145732
  2.7 17.4 %all-to-all-start.1 = ((f32[16,4,128]{2,1,0:T(4,128)}), f32[16,4,128]{2,1,0:T(4,128)S(1)}, u32[]{:S(2)}, u32[]{:S(2)}) async-start(f32[16,4,128]{2,1,0:T(4,128)} %broadcast_in_dim.8), calls=%async_computation.1 | async-start | bytes 65536 | tf_op jit(solution)/shard_map/all_to_all | solution.py:25
  12.7 0.7 copy-start.3
  13.4 0.7 copy-start.4
  42.9 16.5 %copy-start.1 = (f32[1024,128]{1,0:T(8,128)S(1)}, f32[1024,128]{1,0:T(8,128)}, u32[]{:S(2)}) copy-start(f32[1024,128]{1,0:T(8,128)} %sketch_ref.1) | copy-start | bytes 1572868
  61.0 11.5 %all-to-all-start.3 = ((f32[32,8,128]{2,1,0:T(8,128)}), f32[32,8,128]{2,1,0:T(8,128)S(1)}, u32[]{:S(2)}, u32[]{:S(2)}) async-start(f32[32,8,128]{2,1,0:T(8,128)} %get-tuple-element.10), calls=%async_computation.3 | async-start | bytes 262144 | tf_op jit(solution)/shard_map/all_to_all | solution.py:25
  73.2 10.1 %all-to-all-start.4 = ((f32[8,8,128]{2,1,0:T(8,128)}), f32[8,8,128]{2,1,0:T(8,128)S(1)}, u32[]{:S(2)}, u32[]{:S(2)}) async-start(f32[8,8,128]{2,1,0:T(8,128)} %addup.1), calls=%async_computation.4 | async-start | bytes 65536 | tf_op jit(solution)/shard_map/all_to_all | solution.py:25
  83.6 13.8 %copy-start.2 = (f32[8,32,128]{2,1,0:T(8,128)S(1)}, f32[8,32,128]{2,1,0:T(8,128)}, u32[]{:S(2)}) copy-start(f32[8,32,128]{2,1,0:T(8,128)} %krylov_ref.1) | copy-start | bytes 393220

commit v2 on v1

--- a/solution.py
+++ b/solution.py
@@ -13,10 +13,11 @@
 KRYLOV = 8
 FEATS = 32
 LANES = 128
-ALL = ("blk", "grp_0", "grp_1", "grp_2")
-ROW = ("blk", "grp_1")
-COLUMN = ("grp_0", "grp_2")
-OWNERS = ("blk", "grp_1", "grp_2")
+X1, X0, Z2, Z1, Z0, Y1, Y0, CORE = ALL = ("x1", "x0", "z2", "z1", "z0", "y1", "y0", "core")
+COLUMN = (X0, Y1, Y0, CORE)
+ROW = (X1, Z2, Z1, Z0)
+OWNERS = (X1, X0, Y1, Y0, CORE)
+LAYERS = (Z2, Z1, Z0)
 VMEM = pl.BlockSpec(memory_space=pltpu.VMEM)
 MIB = 2**20
 
@@ -25,8 +26,10 @@
     return lax.all_to_all(value, axis, 0, 0, tiled=True)
 
 
-def copies(value, axis):
-    return jnp.broadcast_to(value[None], (lax.axis_size(axis), *value.shape))
+def gather_by_distance(value, axes):
+    for axis in reversed(axes):
+        value = jnp.concatenate([value, lax.ppermute(value, axis, ((0, 1), (1, 0)))], axis=0)
+    return value
 
 
 def parts(value):
@@ -38,6 +41,37 @@
 
 def wide(tiles):
     return jnp.concatenate(tiles, axis=1)
+
+
+def message_kernel(points_ref, labels_ref, scale_ref, vector_ref, sources_ref, targets_ref):
+    for k in range(sources_ref.shape[0]):
+        sources_ref[k, 0:SYSTEMS, :] = vector_ref[0]
+        sources_ref[k, SYSTEMS : SYSTEMS + 3, :] = points_ref[...]
+        sources_ref[k, SYSTEMS + 3 : SYSTEMS + 4, :] = scale_ref[...]
+    targets_ref[0, 0:3, :] = points_ref[...]
+    targets_ref[0, 3:4, :] = labels_ref[...].astype(jnp.float32)
+
+
+def messages(points, labels, shape_scale, krylov, count):
+    last = krylov.shape[0] - 1
+    whole = lambda shape: pl.BlockSpec(shape, lambda i: (0,) * len(shape))
+    return pl.pallas_call(
+        message_kernel,
+        grid=(1,),
+        out_shape=(
+            jax.ShapeDtypeStruct((count, SYSTEMS + 4, LANES), jnp.float32),
+            jax.ShapeDtypeStruct((1, 4, LANES), jnp.float32),
+        ),
+        in_specs=[
+            whole((3, LANES)),
+            whole((1, LANES)),
+            whole((1, LANES)),
+            pl.BlockSpec((1, SYSTEMS, LANES), lambda i: (last, 0, 0)),
+        ],
+        out_specs=(whole((count, SYSTEMS + 4, LANES)), whole((1, 4, LANES))),
+        name="messages",
+        compiler_params=pltpu.CompilerParams(vmem_limit_bytes=4 * MIB),
+    )(points, labels[None, :], shape_scale[None, :], krylov)
 
 
 def pair_kernel(tblock, sblock, source_ref, target_ref, out_ref, source_feats, target_feats, squares, weights):
@@ -68,6 +102,7 @@
     rows += [zero] * (FEATS - len(rows))
     for k, value in enumerate(rows):
         target_feats[:, k, :] = value
+    place = lax.axis_index(COLUMN)
     row = lax.broadcasted_iota(jnp.int32, (FEATS, LANES), 0)
     pick = jnp.where(jnp.logical_and(row >= 24, row < 27), 1.0, 0.0).astype(jnp.bfloat16)
     steps, per, tper = blocks * LANES // sblock, sblock // LANES, tblock // LANES
@@ -106,7 +141,7 @@
             )
         result = total[:SYSTEMS] + total[SYSTEMS:]
         for j in range(tper):
-            out_ref[index * tper + j] = result[:, j * LANES : (j + 1) * LANES]
+            out_ref[jnp.bitwise_xor(place, index * tper + j)] = result[:, j * LANES : (j + 1) * LANES]
         return carry
 
     lax.fori_loop(0, owners // tper, over_targets, 0)
@@ -248,19 +283,19 @@
 
 def shards(points, labels, shape_scale, krylov_basis, sketch, sketched_basis):
     everything = lax.axis_size(ALL) * points.shape[1]
-    sources = jnp.concatenate([krylov_basis[KRYLOV - 1], points, shape_scale[None, :]], axis=0)
-    targets = jnp.concatenate([points, labels[None, :].astype(jnp.float32)], axis=0)
     system = lax.axis_index(OWNERS)
     basis = lax.dynamic_slice_in_dim(sketched_basis, system, 1, axis=1)
     basis = basis.reshape(KRYLOV, -1, LANES)
-    all_targets = exchange(copies(targets, COLUMN), COLUMN)
-    all_sources = exchange(copies(sources, ROW), ROW)
+    sources, targets = messages(points, labels, shape_scale, krylov_basis, lax.axis_size(ROW))
+    all_sources = exchange(sources, ROW)
+    all_targets = gather_by_distance(targets, COLUMN)
+    all_targets, basis = lax.optimization_barrier((all_targets, basis))
     partial_value = pair_product(all_sources, all_targets)
     image, local_sketch = image_and_sketch(
         exchange(partial_value, COLUMN), sketch, math.sqrt(everything)
     )
-    over_owners = sum_for_each(exchange(local_sketch, OWNERS), lax.axis_size("grp_0"))
-    message = project(exchange(over_owners, "grp_0"), basis, lax.axis_size(OWNERS))
+    over_owners = sum_for_each(exchange(local_sketch, OWNERS), lax.axis_size(LAYERS))
+    message = project(exchange(over_owners, LAYERS), basis, lax.axis_size(OWNERS))
     next_vector, coefficients, sketch_next, norms = finish(
         exchange(message, OWNERS), image, krylov_basis
     )
@@ -268,7 +303,7 @@
 
 
 def solution(mesh):
-    torus = Mesh(mesh.devices.reshape(mesh.shape["blk"], 8, 4, 2), ALL)
+    torus = Mesh(mesh.devices.reshape((2,) * len(ALL)), ALL)
     in_specs = (P(None, ALL), P(ALL), P(ALL), P(None, None, ALL), P(None, ALL), P())
     out_specs = (P(None, ALL), P(), P(), P())
     return jax.shard_map(

time: 99 us -> 93.3 us (0.942)
  waiting for transfers between devices: 20.4 us -> 5.87 us
  blocking collectives: 44.8 us -> 56.1 us
  other arithmetic: 1.44 us -> 0.01 us
    all_to_all x3 -> x1, waiting for transfers between devices: 20.4 us -> 0.01 us  [exchange(): return lax.all_to_all(value, axis, 0, 0, tiled=True)]
    all_to_all x3 -> x4, blocking collectives: 44.8 us -> 56.1 us  [exchange(): return lax.all_to_all(value, axis, 0, 0, tiled=True)]
    ppermute x0 -> x4, waiting for transfers between devices: none -> 5.87 us  [gather_by_distance(): lax.ppermute(value, axis, ((0, 1), (1, 0)))]
    all_to_all x3 -> x1, starting transfers between devices: 17.1 us -> 11.6 us  [exchange(): return lax.all_to_all(value, axis, 0, 0, tiled=True)]
    ppermute x0 -> x4, starting transfers between devices: none -> 5.56 us  [gather_by_distance(): lax.ppermute(value, axis, ((0, 1), (1, 0)))]
    unnamed x10 -> x18, local copies, waits for them, and re-layouts: 0.68 us -> 1.7 us
  transfers between devices with their start and end apart: 3 -> 5, of which waited for: 3 -> 4; matrix products, arithmetic and copies ran while one was open for 1% -> 0% of each run, Pallas kernels for 0% -> 0%
where the time goes in v2:
time: 93.3 us; the launch traced here: 92.9 us
  blocking collectives  56.1 us (60%)
  starting transfers between devices  17.1 us (18%)
  Pallas kernels  11.3 us (12%)
  waiting for transfers between devices  5.87 us (6%)
  local copies, waits for them, and re-layouts  1.74 us (2%)
    all_to_all x4, blocking collectives, exchange(): return lax.all_to_all(value, axis, 0, 0, tiled=True)  56.1 us
    all_to_all x1, starting transfers between devices, exchange(): return lax.all_to_all(value, axis, 0, 0, tiled=True)  11.6 us
    pallas_call x1, Pallas kernels, pair_product(): pl.pallas_call(functools.partial(pair_kernel, tblock, sblock), out_shape=...  8.34 us
    ppermute x4, waiting for transfers between devices, gather_by_distance(): lax.ppermute(value, axis, ((0, 1), (1, 0)))  5.87 us
    ppermute x4, starting transfers between devices, gather_by_distance(): lax.ppermute(value, axis, ((0, 1), (1, 0)))  5.56 us
  transfers between devices with their start and end apart: 5, of which 4 were waited for; matrix products, arithmetic and copies ran while one was open for 0% of the time, Pallas kernels for 0%

profile of v2, /device:TPU:1, one launch (start us, length us, event | category | flops | bytes accessed | tf_op | source)
XLA Modules:
  0.0 92.9 jit_solution(5699801742344819760)
XLA Ops:
  0.6 0.0 copy-start
  0.6 0.0 copy-start.4
  0.7 0.0 copy-start.5
  0.7 0.0 copy-start.6
  0.7 0.7 copy-done.4
  1.4 0.0 copy-done.5
  1.4 0.0 copy-done.6
  1.4 0.0 copy-start.1
  1.4 0.9 copy-done.1
  2.3 0.7 messages.1
  3.1 11.6 %all-to-all-start = ((f32[16,36,128]{2,1,0:T(8,128)}), f32[16,36,128]{2,1,0:T(8,128)S(1)}, u32[]{:S(2)}, u32[]{:S(2)}) async-start(f32[16,36,128]{2,1,0:T(8,128)} %get-tuple-element.14), calls=%async_computation | async-start | bytes 655360 | tf_op jit(solution)/shard_map/all_to_all | solution.py:26
  14.6 1.0 %collective-permute-start = (f32[1,4,128]{2,1,0:T(4,128)S(1)}, f32[1,4,128]{2,1,0:T(4,128)S(1)}, u32[]{:S(2)}, u32[]{:S(2)}) collective-permute-start(f32[1,4,128]{2,1,0:T(4,128)S(1)} %get-tuple-element.15), channel_id=1, source_target_pairs={{0,1},{1,0},{2,3},{3,2},{4,5},{5,4},{6,7},{7,6},{8,9},{9,8},{10,11... | collective-permute-start | bytes 6152 | tf_op jit(solution)/shard_map/ppermute | solution.py:31
  15.7 0.0 copy-done
  15.7 0.8 collective-permute-done
  16.5 1.3 %collective-permute-start.1 = (f32[2,4,128]{2,1,0:T(4,128)S(1)}, f32[2,4,128]{2,1,0:T(4,128)S(1)}, u32[]{:S(2)}, u32[]{:S(2)}) collective-permute-start(f32[2,4,128]{2,1,0:T(4,128)S(1)} %pad_maximum_fusion.2), channel_id=1, source_target_pairs={{0,2},{2,0},{1,3},{3,1},{4,6},{6,4},{5,7},{7,5},{8,10},{10,8},{9,1... | collective-permute-start | bytes 12296 | tf_op jit(solution)/shard_map/ppermute | solution.py:31
  17.8 1.2 %collective-permute-done.1 = f32[2,4,128]{2,1,0:T(4,128)S(1)} collective-permute-done((f32[2,4,128]{2,1,0:T(4,128)S(1)}, f32[2,4,128]{2,1,0:T(4,128)S(1)}, u32[]{:S(2)}, u32[]{:S(2)}) %collective-permute-start.1) | collective-permute-done | bytes 4128 | tf_op jit(solution)/shard_map/ppermute | solution.py:31
  19.0 2.9 %collective-permute-start.2 = (f32[4,4,128]{2,1,0:T(4,128)S(1)}, f32[4,4,128]{2,1,0:T(4,128)S(1)}, u32[]{:S(2)}, u32[]{:S(2)}) collective-permute-start(f32[4,4,128]{2,1,0:T(4,128)S(1)} %pad_maximum_fusion.1), channel_id=1, source_target_pairs={{0,4},{4,0},{1,5},{5,1},{2,6},{6,2},{3,7},{7,3},{8,12},{12,8},{9,1... | collective-permute-start | bytes 24584 | tf_op jit(solution)/shard_map/ppermute | solution.py:31
  21.9 1.4 %collective-permute-done.2 = f32[4,4,128]{2,1,0:T(4,128)S(1)} collective-permute-done((f32[4,4,128]{2,1,0:T(4,128)S(1)}, f32[4,4,128]{2,1,0:T(4,128)S(1)}, u32[]{:S(2)}, u32[]{:S(2)}) %collective-permute-start.2) | collective-permute-done | bytes 8224 | tf_op jit(solution)/shard_map/ppermute | solution.py:31
  23.3 0.3 collective-permute-start.3
  23.6 2.6 %collective-permute-done.3 = f32[8,4,128]{2,1,0:T(4,128)S(1)} collective-permute-done((f32[8,4,128]{2,1,0:T(4,128)S(1)}, f32[8,4,128]{2,1,0:T(4,128)S(1)}, u32[]{:S(2)}, u32[]{:S(2)}) %collective-permute-start.3) | collective-permute-done | bytes 16416 | tf_op jit(solution)/shard_map/ppermute | solution.py:31
  26.2 0.0 all-to-all-done.source_ref
  26.2 8.3 %pairs.1 = f32[16,32,128]{2,1,0:T(8,128)S(1)} custom-call(f32[16,36,128]{2,1,0:T(8,128)S(1)} %all-to-all-done.source_ref, f32[16,4,128]{2,1,0:T(4,128)S(1)} %constant_dynamic-update-slice_fusion.target_ref), custom_call_target="tpu_custom_call" | custom-call | flops 805306368 | bytes 1048576 | tf_op jit(solution)/shard_map/pairs/pallas_call | solution.py:153
  34.5 0.0 copy-start.3
  34.5 14.8 %all_to_all.25.arrived_ref = f32[16,32,128]{2,1,0:T(8,128)S(1)} all-to-all(f32[16,32,128]{2,1,0:T(8,128)S(1)} %pairs.1), channel_id=1, replica_groups=mesh['x1'=2,'x0'=2,'z2'=2,'z1'=2,'z0'=2,'y1'=2,'y0'=2,'core'=2] {'x0','y..., dimensions={0} | all-to-all | bytes 524288 | tf_op jit(solution)/shard_map/all_to_all | solution.py:26
  49.4 0.0 copy-done.3
  49.4 0.9 %image.1 = (f32[32,128]{1,0:T(8,128)S(1)}, f32[32,8,128]{2,1,0:T(8,128)S(1)}) custom-call(f32[16,32,128]{2,1,0:T(8,128)S(1)} %all_to_all.25.arrived_ref, f32[1024,128]{1,0:T(8,128)S(1)} %copy-done.3), custom_call_target="tpu_custom_call" | custom-call | tf_op jit(solution)/shard_map/image/pallas_call | solution.py:188
  50.3 14.1 %all_to_all.26.arrived_ref = f32[32,8,128]{2,1,0:T(8,128)S(1)} all-to-all(f32[32,8,128]{2,1,0:T(8,128)S(1)} %get-tuple-element.17), channel_id=1, replica_groups=mesh['x1'=2,'x0'=2,'z2'=2,'z1'=2,'z0'=2,'y1'=2,'y0'=2,'core'=2] {'x1','x..., dimensions={0} | all-to-all | bytes 262144 | tf_op jit(solution)/shard_map/all_to_all | solution.py:26
  64.5 13.1 %all_to_all.27.arrived_ref = f32[8,8,128]{2,1,0:T(8,128)S(1)} all-to-all(f32[8,8,128]{2,1,0:T(8,128)S(1)} %addup.1), channel_id=1, replica_groups=mesh['x1'=2,'x0'=2,'z2'=2,'z1'=2,'z0'=2,'y1'=2,'y0'=2,'core'=2] {'z2','z..., dimensions={0} | all-to-all | bytes 65536 | tf_op jit(solution)/shard_map/all_to_all | solution.py:26
  77.6 0.2 project.1
  77.8 0.0 copy-start.2
  77.8 14.0 %all_to_all.28.arrived_ref = f32[32,16,128]{2,1,0:T(8,128)S(1)} all-to-all(f32[32,16,128]{2,1,0:T(8,128)S(1)} %project.1), channel_id=1, replica_groups=mesh['x1'=2,'x0'=2,'z2'=2,'z1'=2,'z0'=2,'y1'=2,'y0'=2,'core'=2] {'x1','x..., dimensions={0} | all-to-all | bytes 524288 | tf_op jit(solution)/shard_map/all_to_all | solution.py:26
  91.8 0.0 copy-done.2
  91.8 1.1 %finish.1 = (f32[32,128]{1,0:T(8,128)}, f32[8,32]{1,0:T(8,128)}, f32[32,1024]{1,0:T(8,128)}, f32[1,32]{1,0:T(1,128)}) custom-call(f32[32,16,128]{2,1,0:T(8,128)S(1)} %all_to_all.28.arrived_ref, f32[32,128]{1,0:T(8,128)S(1)} %get-tuple-element.19.image_ref, f32[8,32,128]{2,1,0:T(8,128)S(1)} %copy-done.2), custom_call_target="tpu_custom_call" | custom-call | tf_op jit(solution)/shard_map/finish/pallas_call | solution.py:269
  (10 shorter events, 0.1 us)
Async XLA Ops:
  0.6 15.1 %copy-start = (f32[8,32,1024]{2,1,0:T(8,128)S(1)}, f32[8,32,1024]{2,1,0:T(8,128)}, u32[]{:S(2)}) copy-start(f32[8,32,1024]{2,1,0:T(8,128)} %param.11) | copy-start | bytes 3145732
  0.6 0.8 copy-start.4
  0.7 0.8 copy-start.5
  0.7 0.8 copy-start.6
  1.4 0.9 copy-start.1
  3.1 23.1 %all-to-all-start = ((f32[16,36,128]{2,1,0:T(8,128)}), f32[16,36,128]{2,1,0:T(8,128)S(1)}, u32[]{:S(2)}, u32[]{:S(2)}) async-start(f32[16,36,128]{2,1,0:T(8,128)} %get-tuple-element.14), calls=%async_computation | async-start | bytes 655360 | tf_op jit(solution)/shard_map/all_to_all | solution.py:26
  14.6 1.9 %collective-permute-start = (f32[1,4,128]{2,1,0:T(4,128)S(1)}, f32[1,4,128]{2,1,0:T(4,128)S(1)}, u32[]{:S(2)}, u32[]{:S(2)}) collective-permute-start(f32[1,4,128]{2,1,0:T(4,128)S(1)} %get-tuple-element.15), channel_id=1, source_target_pairs={{0,1},{1,0},{2,3},{3,2},{4,5},{5,4},{6,7},{7,6},{8,9},{9,8},{10,11... | collective-permute-start | bytes 6152 | tf_op jit(solution)/shard_map/ppermute | solution.py:31
  16.5 2.5 %collective-permute-start.1 = (f32[2,4,128]{2,1,0:T(4,128)S(1)}, f32[2,4,128]{2,1,0:T(4,128)S(1)}, u32[]{:S(2)}, u32[]{:S(2)}) collective-permute-start(f32[2,4,128]{2,1,0:T(4,128)S(1)} %pad_maximum_fusion.2), channel_id=1, source_target_pairs={{0,2},{2,0},{1,3},{3,1},{4,6},{6,4},{5,7},{7,5},{8,10},{10,8},{9,1... | collective-permute-start | bytes 12296 | tf_op jit(solution)/shard_map/ppermute | solution.py:31
  19.0 4.3 %collective-permute-start.2 = (f32[4,4,128]{2,1,0:T(4,128)S(1)}, f32[4,4,128]{2,1,0:T(4,128)S(1)}, u32[]{:S(2)}, u32[]{:S(2)}) collective-permute-start(f32[4,4,128]{2,1,0:T(4,128)S(1)} %pad_maximum_fusion.1), channel_id=1, source_target_pairs={{0,4},{4,0},{1,5},{5,1},{2,6},{6,2},{3,7},{7,3},{8,12},{12,8},{9,1... | collective-permute-start | bytes 24584 | tf_op jit(solution)/shard_map/ppermute | solution.py:31
  23.3 2.9 %collective-permute-start.3 = (f32[8,4,128]{2,1,0:T(4,128)S(1)}, f32[8,4,128]{2,1,0:T(4,128)S(1)}, u32[]{:S(2)}, u32[]{:S(2)}) collective-permute-start(f32[8,4,128]{2,1,0:T(4,128)S(1)} %pad_maximum_fusion), channel_id=1, source_target_pairs={{0,64},{64,0},{1,65},{65,1},{2,66},{66,2},{3,67},{67,3},{4,68},{68... | collective-permute-start | bytes 49160 | tf_op jit(solution)/shard_map/ppermute | solution.py:31
  34.5 14.8 %copy-start.3 = (f32[1024,128]{1,0:T(8,128)S(1)}, f32[1024,128]{1,0:T(8,128)}, u32[]{:S(2)}) copy-start(f32[1024,128]{1,0:T(8,128)} %sketch_ref.1) | copy-start | bytes 1572868
  77.8 14.0 %copy-start.2 = (f32[8,32,128]{2,1,0:T(8,128)S(1)}, f32[8,32,128]{2,1,0:T(8,128)}, u32[]{:S(2)}) copy-start(f32[8,32,128]{2,1,0:T(8,128)} %krylov_ref.1) | copy-start | bytes 393220

commit v3 on v2

v3 whole, which is shorter than its diff:
```python
import functools
import math

import jax
import jax.numpy as jnp
from jax import lax
from jax.experimental import pallas as pl
from jax.experimental.pallas import tpu as pltpu
from jax.sharding import Mesh
from jax.sharding import PartitionSpec as P

SYSTEMS = 32
KRYLOV = 8
FEATS = 32
LANES = 128
X1, X0, Z2, Z1, Z0, Y1, Y0, CORE = ALL = ("x1", "x0", "z2", "z1", "z0", "y1", "y0", "core")
COLUMN = (Z1, Z0, Z2)
ROW = (X1, X0, Y1, Y0)
OWNERS = (X1, X0, Y1, Y0, CORE)
LAYERS = (Z2, Z1, Z0)
VMEM = pl.BlockSpec(memory_space=pltpu.VMEM)
MIB = 2**20


def exchange(value, axis):
    return lax.all_to_all(value, axis, 0, 0, tiled=True)


def swap(value, axis):
    return lax.ppermute(value, axis, ((0, 1), (1, 0)))


def gather_by_distance(value, axes):
    value = jnp.concatenate([value, swap(value, axes[-1])], axis=0)
    value = jnp.concatenate([value, swap(value, axes[-2])], axis=0)
    for axis in reversed(axes[:-2]):
        value = jnp.concatenate([value, swap(value, axis)], axis=0)
    return value


def parts(value):
    first = value.astype(jnp.bfloat16).astype(jnp.float32)
    rest = value - first
    second = rest.astype(jnp.bfloat16).astype(jnp.float32)
    return [first, second, rest - second]


def wide(tiles):
    return jnp.concatenate(tiles, axis=1)


def message_kernel(points_ref, labels_ref, scale_ref, krylov_ref, sources_ref, targets_ref, vector, row, copied, sem):
    taken = [
        pltpu.make_async_copy(krylov_ref.at[krylov_ref.shape[0] - 1], vector, sem.at[0]),
        pltpu.make_async_copy(points_ref, row.at[0:3], sem.at[1]),
        pltpu.make_async_copy(scale_ref, row.at[3:4], sem.at[2]),
        pltpu.make_async_copy(labels_ref, copied, sem.at[3]),
    ]
    for copy in taken:
        copy.start()
    for copy in taken:
        copy.wait()
    for k in range(sources_ref.shape[0]):
        sources_ref[k, 0:SYSTEMS, :] = vector[...]
        sources_ref[k, SYSTEMS : SYSTEMS + 4, :] = row[...]
    targets_ref[0, 0:3, :] = row[0:3, :]
    targets_ref[0, 3:4, :] = copied[...].astype(jnp.float32)


def messages(points, labels, shape_scale, krylov, count):
    hbm = pl.BlockSpec(memory_space=pltpu.HBM)
    return pl.pallas_call(
        message_kernel,
        out_shape=(
            jax.ShapeDtypeStruct((count, SYSTEMS + 4, LANES), jnp.float32),
            jax.ShapeDtypeStruct((1, 4, LANES), jnp.float32),
        ),
        in_specs=[hbm] * 4,
        out_specs=(VMEM,) * 2,
        scratch_shapes=[
            pltpu.VMEM((SYSTEMS, LANES), jnp.float32),
            pltpu.VMEM((4, LANES), jnp.float32),
            pltpu.VMEM((1, LANES), jnp.int32),
            pltpu.SemaphoreType.DMA((4,)),
        ],
        name="messages",
    )(points, labels[None, :], shape_scale[None, :], krylov)


def stored(rows, count, out_ref):
    zero = jnp.zeros((count, LANES), jnp.float32)
    for k, value in enumerate(rows + [zero] * (FEATS - len(rows))):
        out_ref[:, k, :] = value


def pair_kernel(unroll, *refs):
    (*source_refs, target_ref, out_ref, source_feats, target_feats, weights) = refs
    before_ref = None
    if len(source_refs) > 1:
        (*source_refs, before_ref) = source_refs
    for number, source_ref in enumerate(source_refs):
        count = source_ref.shape[0]
        coords = [source_ref[:, SYSTEMS + a, :] - 0.5 for a in range(3)]
        scale = source_ref[:, SYSTEMS + 3, :]
        per_square = 1.0 / (scale * scale)
        rows = []
        for value in [c * per_square for c in coords] + [per_square]:
            a, b, c = parts(value)
            rows += [a, a, b, b, a, c]
        square = coords[0] * coords[0] + coords[1] * coords[1] + coords[2] * coords[2]
        rows += parts(square * per_square + 1.0)
        stored(rows, count, source_feats.at[number * count : (number + 1) * count])
        for step in range(count // 2):
            weight = wide([source_ref[2 * step + j, 0:SYSTEMS, :] for j in range(2)])
            scale = wide([source_ref[2 * step + j, SYSTEMS + 3 : SYSTEMS + 4, :] for j in range(2)])
            inner, outer = weight / scale, weight * scale
            terms = []
            for value in (inner, outer):
                first = value.astype(jnp.bfloat16)
                terms += [first, (value - first.astype(jnp.float32)).astype(jnp.bfloat16)]
            weights[number * (count // 2) + step] = jnp.concatenate(terms, axis=0)
    owners = target_ref.shape[0]
    coords = [target_ref[:, a, :] - 0.5 for a in range(3)]
    square = coords[0] * coords[0] + coords[1] * coords[1] + coords[2] * coords[2]
    rows = []
    for value in [-2.0 * c for c in coords] + [square]:
        a, b, c = parts(value)
        rows += [a, b, a, b, c, a]
    rows += [jnp.ones((owners, LANES), jnp.float32)] * 3
    stored(rows, owners, target_feats)
    place = lax.axis_index(COLUMN)
    over_rows = (((0,), (0,)), ((), ()))

    def feats_of(ref, step):
        return wide([ref[2 * step], ref[2 * step + 1]]).astype(jnp.bfloat16)

    def over_targets(start, carry):
        for index in [start * unroll + k for k in range(unroll)]:
            feats = feats_of(target_feats, index)
            inner = wide([target_ref[2 * index + j, 3:4, :] for j in range(2)]) > 0.5
            total = jnp.zeros((4 * SYSTEMS, 2 * LANES), jnp.float32)
            for step in range(weights.shape[0]):
                ratio = lax.dot_general(
                    feats_of(source_feats, step), feats, over_rows, preferred_element_type=jnp.float32
                )
                root = lax.rsqrt(ratio)
                kernel = root * jnp.where(inner, 2.0 + root * root, ratio)
                first = kernel.astype(jnp.bfloat16)
                second = (kernel - first.astype(jnp.float32)).astype(jnp.bfloat16)
                weight = weights[step]
                total = (
                    total
                    + jnp.dot(weight, first, preferred_element_type=jnp.float32)
                    + jnp.dot(weight, second, preferred_element_type=jnp.float32)
                )
            a, b, c, d = (total[k * SYSTEMS : (k + 1) * SYSTEMS] for k in range(4))
            result = jnp.where(inner, a + b, c + d)
            for j in range(2):
                owner = jnp.bitwise_xor(place, 2 * index + j)
                part = result[:, j * LANES : (j + 1) * LANES]
                out_ref[owner] = part if before_ref is None else part + before_ref[owner]
        return carry

    lax.fori_loop(0, owners // 2 // unroll, over_targets, 0)


def pair_product(sources, targets, unroll=2):
    blocks, owners = sources[0].shape[0], targets.shape[0]
    pairs = blocks * owners * LANES * LANES
    return pl.pallas_call(
        functools.partial(pair_kernel, unroll),
        out_shape=jax.ShapeDtypeStruct((owners, SYSTEMS, LANES), jnp.float32),
        in_specs=[VMEM] * (len(sources) + 1),
        out_specs=VMEM,
        scratch_shapes=[
            pltpu.VMEM((blocks, FEATS, LANES), jnp.float32),
            pltpu.VMEM((owners, FEATS, LANES), jnp.float32),
            pltpu.VMEM((blocks // 2, 4 * SYSTEMS, 2 * LANES), jnp.bfloat16),
        ],
        cost_estimate=pl.CostEstimate(flops=6 * SYSTEMS * pairs, bytes_accessed=2**20, transcendentals=pairs),
        name="pairs",
        compiler_params=pltpu.CompilerParams(vmem_limit_bytes=16 * MIB),
    )(*sources, targets)


def image_kernel(root, arrived_ref, sketch_ref, image_ref, local_ref):
    total = arrived_ref[0]
    for k in range(1, arrived_ref.shape[0]):
        total = total + arrived_ref[k]
    image = total / root
    image_ref[...] = image
    for k in range(sketch_ref.shape[0] // LANES):
        local_ref[:, k, :] = lax.dot_general(
            image,
            sketch_ref[k * LANES : (k + 1) * LANES, :],
            (((1,), (1,)), ((), ())),
            precision=lax.Precision.HIGHEST,
            preferred_element_type=jnp.float32,
        )


def image_and_sketch(arrived, sketch, root):
    rows = sketch.shape[0]
    return pl.pallas_call(
        functools.partial(image_kernel, root),
        out_shape=(
            jax.ShapeDtypeStruct((SYSTEMS, LANES), jnp.float32),
            jax.ShapeDtypeStruct((SYSTEMS, rows // LANES, LANES), jnp.float32),
        ),
        in_specs=[VMEM] * 2,
        out_specs=(VMEM,) * 2,
        name="image",
        compiler_params=pltpu.CompilerParams(vmem_limit_bytes=8 * MIB),
    )(arrived, sketch)


def sum_kernel(arrived_ref, out_ref):
    total = arrived_ref[0]
    for k in range(1, arrived_ref.shape[0]):
        total = total + arrived_ref[k]
    for k in range(out_ref.shape[0]):
        out_ref[k] = total


def sum_for_each(arrived, count):
    return pl.pallas_call(
        sum_kernel,
        out_shape=jax.ShapeDtypeStruct((count, *arrived.shape[1:]), jnp.float32),
        in_specs=[VMEM],
        out_specs=VMEM,
        name="addup",
        compiler_params=pltpu.CompilerParams(vmem_limit_bytes=4 * MIB),
    )(arrived)


def project_kernel(arrived_ref, basis_ref, out_ref):
    sketched = arrived_ref[0]
    for k in range(1, arrived_ref.shape[0]):
        sketched = sketched + arrived_ref[k]
    lane = lax.broadcasted_iota(jnp.int32, (8, LANES), 1)

    def whole(value):
        return jnp.sum(jnp.sum(value, axis=1, keepdims=True), axis=0, keepdims=True)

    scalars = jnp.zeros((8, LANES), jnp.float32)
    remainder = sketched
    for j in range(KRYLOV):
        coefficient = whole(basis_ref[j] * sketched)
        scalars = jnp.where(lane == j, coefficient, scalars)
        remainder = remainder - coefficient * basis_ref[j]
    norm = jnp.sqrt(whole(remainder * remainder) / (sketched.shape[0] * LANES) + 1e-06)
    scalars = jnp.where(lane == KRYLOV, norm, scalars)
    message = jnp.concatenate([remainder / norm, scalars], axis=0)
    for k in range(out_ref.shape[0]):
        out_ref[k] = message


def project(arrived, basis, count):
    return pl.pallas_call(
        project_kernel,
        out_shape=jax.ShapeDtypeStruct((count, arrived.shape[1] + 8, LANES), jnp.float32),
        in_specs=[VMEM] * 2,
        out_specs=VMEM,
        name="project",
        compiler_params=pltpu.CompilerParams(vmem_limit_bytes=4 * MIB),
    )(arrived, basis)


def finish_kernel(arrived_ref, image_ref, krylov_ref, next_ref, coefficients_ref, sketch_ref, norms_ref):
    rows = arrived_ref.shape[1] - 8
    for k in range(rows):
        sketch_ref[:, k * LANES : (k + 1) * LANES] = arrived_ref[:, k, :]
    scalars = arrived_ref[:, rows, :]
    reduced = image_ref[...]
    for j in range(KRYLOV):
        reduced = reduced - scalars[:, j : j + 1] * krylov_ref[j]
    next_ref[...] = reduced / scalars[:, KRYLOV : KRYLOV + 1]
    across = jnp.transpose(scalars)
    coefficients_ref[...] = across[0:KRYLOV, :]
    norms_ref[...] = across[KRYLOV : KRYLOV + 1, :]


def finish(arrived, image, krylov):
    rows = arrived.shape[1] - 8
    return pl.pallas_call(
        finish_kernel,
        out_shape=(
            jax.ShapeDtypeStruct((SYSTEMS, LANES), jnp.float32),
            jax.ShapeDtypeStruct((KRYLOV, SYSTEMS), jnp.float32),
            jax.ShapeDtypeStruct((SYSTEMS, rows * LANES), jnp.float32),
            jax.ShapeDtypeStruct((1, SYSTEMS), jnp.float32),
        ),
        in_specs=[VMEM] * 3,
        out_specs=(VMEM,) * 4,
        name="finish",
        compiler_params=pltpu.CompilerParams(vmem_limit_bytes=8 * MIB),
    )(arrived, image, krylov)


def step(points, labels, shape_scale, krylov_basis, sketch, sketched_basis):
    everything = lax.axis_size(ALL) * points.shape[1]
    system = lax.axis_index(OWNERS)
    basis = lax.dynamic_slice_in_dim(sketched_basis, system, 1, axis=1)
    basis = basis.reshape(KRYLOV, -1, LANES)
    sources, targets = messages(points, labels, shape_scale, krylov_basis, lax.axis_size(ROW))
    all_sources = exchange(sources, ROW)
    all_targets = gather_by_distance(targets, COLUMN)
    all_targets, all_sources, basis = lax.optimization_barrier((all_targets, all_sources, basis))
    other_sources = swap(all_sources, CORE)
    partial_value = pair_product((all_sources,), all_targets)
    partial_value = pair_product((other_sources, partial_value), all_targets)
    image, local_sketch = image_and_sketch(
        exchange(partial_value, COLUMN), sketch, math.sqrt(everything)
    )
    over_owners = sum_for_each(exchange(local_sketch, OWNERS), lax.axis_size(LAYERS))
    message = project(exchange(over_owners, LAYERS), basis, lax.axis_size(OWNERS))
    next_vector, coefficients, sketch_next, norms = finish(
        exchange(message, OWNERS), image, krylov_basis
    )
    return (next_vector, coefficients, sketch_next, norms.reshape(-1))


def solution(mesh):
    torus = Mesh(mesh.devices.reshape((2,) * len(ALL)), ALL)
    in_specs = (P(None, ALL), P(ALL), P(ALL), P(None, None, ALL), P(None, ALL), P())
    out_specs = (P(None, ALL), P(), P(), P())
    return jax.shard_map(step, mesh=torus, in_specs=in_specs, out_specs=out_specs, check_vma=False)
```

time: 93.3 us -> 90 us (0.965)
  blocking collectives: 56.1 us -> 50.3 us
  starting transfers between devices: 17.1 us -> 20.9 us
  local copies, waits for them, and re-layouts: 1.74 us -> 0.72 us
    ppermute x4, starting transfers between devices: 5.56 us -> 14.2 us  [swap(): return lax.ppermute(value, axis, ((0, 1), (1, 0)))]
    all_to_all x4, blocking collectives: 56.1 us -> 50.3 us  [exchange(): return lax.all_to_all(value, axis, 0, 0, tiled=True)]
    all_to_all x1, starting transfers between devices: 11.6 us -> 6.75 us  [exchange(): return lax.all_to_all(value, axis, 0, 0, tiled=True)]
    ppermute x4, waiting for transfers between devices: 5.87 us -> 2.22 us  [swap(): return lax.ppermute(value, axis, ((0, 1), (1, 0)))]
    all_to_all x1, waiting for transfers between devices: 0.01 us -> 3.56 us  [exchange(): return lax.all_to_all(value, axis, 0, 0, tiled=True)]
    unnamed x18 -> x8, local copies, waits for them, and re-layouts: 1.7 us -> 0.69 us
    pallas_call x2 -> x3, Pallas kernels: 9.08 us -> 8.17 us  [the longest x2 6.57 us: pair_product(): pl.pallas_call(functools.partial(pair_kernel, unroll), out_shape=jax.Shap...]
  transfers between devices with their start and end apart: 5 -> 5, of which waited for: 4 -> 3; matrix products, arithmetic and copies ran while one was open for 0% -> 0% of each run, Pallas kernels for 0% -> 4%
where the time goes in v3:
time: 90 us; the launch traced here: 89.6 us
  blocking collectives  50.3 us (56%)
  starting transfers between devices  20.9 us (23%)
  Pallas kernels  10.4 us (12%)
  waiting for transfers between devices  5.78 us (6%)
    all_to_all x4, blocking collectives, exchange(): return lax.all_to_all(value, axis, 0, 0, tiled=True)  50.3 us
    ppermute x4, starting transfers between devices, swap(): return lax.ppermute(value, axis, ((0, 1), (1, 0)))  14.2 us
    all_to_all x1, starting transfers between devices, exchange(): return lax.all_to_all(value, axis, 0, 0, tiled=True)  6.75 us
    pallas_call x2, Pallas kernels, pair_product(): pl.pallas_call(functools.partial(pair_kernel, unroll), out_shape=jax.Shap...  6.57 us
    all_to_all x1, waiting for transfers between devices, exchange(): return lax.all_to_all(value, axis, 0, 0, tiled=True)  3.56 us
    ppermute x4, waiting for transfers between devices, swap(): return lax.ppermute(value, axis, ((0, 1), (1, 0)))  2.22 us
  transfers between devices with their start and end apart: 5, of which 3 were waited for; matrix products, arithmetic and copies ran while one was open for 0% of the time, Pallas kernels for 4%

profile of v3, /device:TPU:1, one launch (start us, length us, event | category | flops | bytes accessed | tf_op | source)
XLA Modules:
  0.0 89.6 jit_solution(12824418380798246348)
XLA Ops:
  0.6 0.0 copy-start
  0.6 1.6 %messages.1 = (f32[16,36,128]{2,1,0:T(8,128)}, f32[1,4,128]{2,1,0:T(4,128)}) custom-call(f32[3,128]{1,0:T(4,128)} %points_ref.1, s32[1,128]{1,0:T(1,128)} %bitcast.5, f32[1,128]{1,0:T(1,128)} %bitcast.6, f32[8,32,128]{2,1,0:T(8,128)} %krylov_ref.3), custom_call_target="tpu_custom_call" | custom-call | tf_op jit(solution)/shard_map/messages/pallas_call | solution.py:72
  2.2 7.8 %collective-permute-start = (f32[1,4,128]{2,1,0:T(4,128)}, f32[1,4,128]{2,1,0:T(4,128)S(1)}, u32[]{:S(2)}, u32[]{:S(2)}) collective-permute-start(f32[1,4,128]{2,1,0:T(4,128)} %get-tuple-element.15), channel_id=1, source_target_pairs={{0,32},{32,0},{1,33},{33,1},{2,34},{34,2},{3,35},{35,3},{4,36},{36... | collective-permute-start | bytes 6152 | tf_op jit(solution)/shard_map/ppermute | solution.py:30
  10.1 1.2 %collective-permute-done = f32[1,4,128]{2,1,0:T(4,128)S(1)} collective-permute-done((f32[1,4,128]{2,1,0:T(4,128)}, f32[1,4,128]{2,1,0:T(4,128)S(1)}, u32[]{:S(2)}, u32[]{:S(2)}) %collective-permute-start) | collective-permute-done | bytes 2080 | tf_op jit(solution)/shard_map/ppermute | solution.py:30
  11.2 0.7 pad_maximum_fusion.2
  11.9 0.7 collective-permute-start.1
  12.7 6.8 %all-to-all-start = ((f32[16,36,128]{2,1,0:T(8,128)}), f32[16,36,128]{2,1,0:T(8,128)S(1)}, u32[]{:S(2)}, u32[]{:S(2)}) async-start(f32[16,36,128]{2,1,0:T(8,128)} %get-tuple-element.16), calls=%async_computation | async-start | bytes 655360 | tf_op jit(solution)/shard_map/all_to_all | solution.py:26
  19.4 0.0 copy-start.3
  19.5 0.0 collective-permute-done.1
  19.5 0.7 copy-done.3
  20.1 2.3 %collective-permute-start.2 = (f32[4,4,128]{2,1,0:T(4,128)S(1)}, f32[4,4,128]{2,1,0:T(4,128)S(1)}, u32[]{:S(2)}, u32[]{:S(2)}) collective-permute-start(f32[4,4,128]{2,1,0:T(4,128)S(1)} %pad_maximum_fusion.1), channel_id=1, source_target_pairs={{0,16},{16,0},{1,17},{17,1},{2,18},{18,2},{3,19},{19,3},{4,20},{20... | collective-permute-start | bytes 24584 | tf_op jit(solution)/shard_map/ppermute | solution.py:30
  22.5 0.0 copy-done
  22.5 1.0 %collective-permute-done.2 = f32[4,4,128]{2,1,0:T(4,128)S(1)} collective-permute-done((f32[4,4,128]{2,1,0:T(4,128)S(1)}, f32[4,4,128]{2,1,0:T(4,128)S(1)}, u32[]{:S(2)}, u32[]{:S(2)}) %collective-permute-start.2) | collective-permute-done | bytes 8224 | tf_op jit(solution)/shard_map/ppermute | solution.py:30
  23.5 3.6 %all-to-all-done.refs_0_ = f32[16,36,128]{2,1,0:T(8,128)S(1)} async-done(((f32[16,36,128]{2,1,0:T(8,128)}), f32[16,36,128]{2,1,0:T(8,128)S(1)}, u32[]{:S(2)}, u32[]{:S(2)}) %all-to-all-start) | async-done | bytes 294944 | tf_op jit(solution)/shard_map/all_to_all | solution.py:26
  27.1 3.3 %collective-permute-start.3 = (f32[16,36,128]{2,1,0:T(8,128)S(1)}, f32[16,36,128]{2,1,0:T(8,128)S(1)}, u32[]{:S(2)}, u32[]{:S(2)}) collective-permute-start(f32[16,36,128]{2,1,0:T(8,128)S(1)} %all-to-all-done.refs_0_), channel_id=1, source_target_pairs={{0,1},{1,0},{2,3},{3,2},{4,5},{5,4},{6,7},{7,6},{8,9},{9,8},{10,11... | collective-permute-start | bytes 884744 | tf_op jit(solution)/shard_map/ppermute | solution.py:30
  30.4 3.3 %pairs.2.refs_1_ = f32[8,32,128]{2,1,0:T(8,128)S(1)} custom-call(f32[16,36,128]{2,1,0:T(8,128)S(1)} %all-to-all-done.refs_0_, f32[8,4,128]{2,1,0:T(4,128)S(1)} %pad_maximum_fusion.refs_1_.refs_2_), custom_call_target="tpu_custom_call" | custom-call | flops 402653184 | bytes 1048576 | tf_op jit(solution)/shard_map/pairs/pallas_call | solution.py:170
  33.6 0.0 collective-permute-done.3.refs_0_
  33.7 0.0 copy-start.1
  33.7 3.3 %pairs.3 = f32[8,32,128]{2,1,0:T(8,128)S(1)} custom-call(f32[16,36,128]{2,1,0:T(8,128)S(1)} %collective-permute-done.3.refs_0_, f32[8,32,128]{2,1,0:T(8,128)S(1)} %pairs.2.refs_1_, f32[8,4,128]{2,1,0:T(4,128)S(1)} %pad_maximum_fusion.refs_1_.refs_2_), custom_call_target="tpu_custom_call" | custom-call | flops 402653184 | bytes 1048576 | tf_op jit(solution)/shard_map/pairs/pallas_call | solution.py:170
  37.0 13.5 %all_to_all.25.arrived_ref = f32[8,32,128]{2,1,0:T(8,128)S(1)} all-to-all(f32[8,32,128]{2,1,0:T(8,128)S(1)} %pairs.3), channel_id=1, replica_groups=mesh['x1'=2,'x0'=2,'z2'=2,'z1'=2,'z0'=2,'y1'=2,'y0'=2,'core'=2] {'z1','z..., dimensions={0} | all-to-all | bytes 262144 | tf_op jit(solution)/shard_map/all_to_all | solution.py:26
  50.5 0.0 copy-done.1
  50.5 0.9 %image.1 = (f32[32,128]{1,0:T(8,128)S(1)}, f32[32,8,128]{2,1,0:T(8,128)S(1)}) custom-call(f32[8,32,128]{2,1,0:T(8,128)S(1)} %all_to_all.25.arrived_ref, f32[1024,128]{1,0:T(8,128)S(1)} %copy-done.1), custom_call_target="tpu_custom_call" | custom-call | tf_op jit(solution)/shard_map/image/pallas_call | solution.py:204
  51.5 13.0 %all_to_all.26.arrived_ref = f32[32,8,128]{2,1,0:T(8,128)S(1)} all-to-all(f32[32,8,128]{2,1,0:T(8,128)S(1)} %get-tuple-element.19), channel_id=1, replica_groups=mesh['x1'=2,'x0'=2,'z2'=2,'z1'=2,'z0'=2,'y1'=2,'y0'=2,'core'=2] {'x1','x..., dimensions={0} | all-to-all | bytes 262144 | tf_op jit(solution)/shard_map/all_to_all | solution.py:26
  64.5 9.8 %all_to_all.27.arrived_ref = f32[8,8,128]{2,1,0:T(8,128)S(1)} all-to-all(f32[8,8,128]{2,1,0:T(8,128)S(1)} %addup.1), channel_id=1, replica_groups=mesh['x1'=2,'x0'=2,'z2'=2,'z1'=2,'z0'=2,'y1'=2,'y0'=2,'core'=2] {'z2','z..., dimensions={0} | all-to-all | bytes 65536 | tf_op jit(solution)/shard_map/all_to_all | solution.py:26
  74.3 0.2 project.1
  74.5 0.0 copy-start.2
  74.5 14.0 %all_to_all.28.arrived_ref = f32[32,16,128]{2,1,0:T(8,128)S(1)} all-to-all(f32[32,16,128]{2,1,0:T(8,128)S(1)} %project.1), channel_id=1, replica_groups=mesh['x1'=2,'x0'=2,'z2'=2,'z1'=2,'z0'=2,'y1'=2,'y0'=2,'core'=2] {'x1','x..., dimensions={0} | all-to-all | bytes 524288 | tf_op jit(solution)/shard_map/all_to_all | solution.py:26
  88.5 0.0 copy-done.2
  88.5 1.1 %finish.1 = (f32[32,128]{1,0:T(8,128)}, f32[8,32]{1,0:T(8,128)}, f32[32,1024]{1,0:T(8,128)}, f32[1,32]{1,0:T(1,128)}) custom-call(f32[32,16,128]{2,1,0:T(8,128)S(1)} %all_to_all.28.arrived_ref, f32[32,128]{1,0:T(8,128)S(1)} %get-tuple-element.21.image_ref, f32[8,32,128]{2,1,0:T(8,128)S(1)} %copy-done.2), custom_call_target="tpu_custom_call" | custom-call | tf_op jit(solution)/shard_map/finish/pallas_call | solution.py:285
  (4 shorter events, 0.1 us)
Async XLA Ops:
  0.6 21.9 %copy-start = (f32[8,32,1024]{2,1,0:T(8,128)S(1)}, f32[8,32,1024]{2,1,0:T(8,128)}, u32[]{:S(2)}) copy-start(f32[8,32,1024]{2,1,0:T(8,128)} %param.11) | copy-start | bytes 3145732
  2.2 9.0 %collective-permute-start = (f32[1,4,128]{2,1,0:T(4,128)}, f32[1,4,128]{2,1,0:T(4,128)S(1)}, u32[]{:S(2)}, u32[]{:S(2)}) collective-permute-start(f32[1,4,128]{2,1,0:T(4,128)} %get-tuple-element.15), channel_id=1, source_target_pairs={{0,32},{32,0},{1,33},{33,1},{2,34},{34,2},{3,35},{35,3},{4,36},{36... | collective-permute-start | bytes 6152 | tf_op jit(solution)/shard_map/ppermute | solution.py:30
  11.9 7.5 %collective-permute-start.1 = (f32[2,4,128]{2,1,0:T(4,128)S(1)}, f32[2,4,128]{2,1,0:T(4,128)S(1)}, u32[]{:S(2)}, u32[]{:S(2)}) collective-permute-start(f32[2,4,128]{2,1,0:T(4,128)S(1)} %pad_maximum_fusion.2), channel_id=1, source_target_pairs={{0,8},{8,0},{1,9},{9,1},{2,10},{10,2},{3,11},{11,3},{4,12},{12,4},... | collective-permute-start | bytes 12296 | tf_op jit(solution)/shard_map/ppermute | solution.py:30
  12.7 14.4 %all-to-all-start = ((f32[16,36,128]{2,1,0:T(8,128)}), f32[16,36,128]{2,1,0:T(8,128)S(1)}, u32[]{:S(2)}, u32[]{:S(2)}) async-start(f32[16,36,128]{2,1,0:T(8,128)} %get-tuple-element.16), calls=%async_computation | async-start | bytes 655360 | tf_op jit(solution)/shard_map/all_to_all | solution.py:26
  19.4 0.7 copy-start.3
  20.1 3.4 %collective-permute-start.2 = (f32[4,4,128]{2,1,0:T(4,128)S(1)}, f32[4,4,128]{2,1,0:T(4,128)S(1)}, u32[]{:S(2)}, u32[]{:S(2)}) collective-permute-start(f32[4,4,128]{2,1,0:T(4,128)S(1)} %pad_maximum_fusion.1), channel_id=1, source_target_pairs={{0,16},{16,0},{1,17},{17,1},{2,18},{18,2},{3,19},{19,3},{4,20},{20... | collective-permute-start | bytes 24584 | tf_op jit(solution)/shard_map/ppermute | solution.py:30
  27.1 6.5 %collective-permute-start.3 = (f32[16,36,128]{2,1,0:T(8,128)S(1)}, f32[16,36,128]{2,1,0:T(8,128)S(1)}, u32[]{:S(2)}, u32[]{:S(2)}) collective-permute-start(f32[16,36,128]{2,1,0:T(8,128)S(1)} %all-to-all-done.refs_0_), channel_id=1, source_target_pairs={{0,1},{1,0},{2,3},{3,2},{4,5},{5,4},{6,7},{7,6},{8,9},{9,8},{10,11... | collective-permute-start | bytes 884744 | tf_op jit(solution)/shard_map/ppermute | solution.py:30
  33.7 16.9 %copy-start.1 = (f32[1024,128]{1,0:T(8,128)S(1)}, f32[1024,128]{1,0:T(8,128)}, u32[]{:S(2)}) copy-start(f32[1024,128]{1,0:T(8,128)} %sketch_ref.1) | copy-start | bytes 1572868
  74.5 14.0 %copy-start.2 = (f32[8,32,128]{2,1,0:T(8,128)S(1)}, f32[8,32,128]{2,1,0:T(8,128)}, u32[]{:S(2)}) copy-start(f32[8,32,128]{2,1,0:T(8,128)} %krylov_ref.3) | copy-start | bytes 393220

commit v4 on v3

v4 whole, which is shorter than its diff:
```python
import functools
import math

import jax
import jax.numpy as jnp
from jax import lax
from jax.experimental import pallas as pl
from jax.experimental.pallas import tpu as pltpu
from jax.sharding import Mesh
from jax.sharding import PartitionSpec as P

SYSTEMS = 32
KRYLOV = 8
FEATS = 32
LANES = 128
X1, X0, Z2, Z1, Z0, Y1, Y0, CORE = ALL = ("x1", "x0", "z2", "z1", "z0", "y1", "y0", "core")
COLUMN = (Z2, Z0, Z1)
ROW = (X1, X0, Y1, Y0)
OWNERS = (X1, X0, Y1, Y0, CORE)
LAYERS = (Z2, Z1, Z0)
VMEM = pl.BlockSpec(memory_space=pltpu.VMEM)
MIB = 2**20


def exchange(value, axis):
    return lax.all_to_all(value, axis, 0, 0, tiled=True)


def swap(value, axis):
    return lax.ppermute(value, axis, ((0, 1), (1, 0)))


def with_other(value, axis):
    return jnp.concatenate([value, swap(value, axis)], axis=0)


def parts(value):
    first = value.astype(jnp.bfloat16).astype(jnp.float32)
    rest = value - first
    second = rest.astype(jnp.bfloat16).astype(jnp.float32)
    return [first, second, rest - second]


def wide(tiles):
    return jnp.concatenate(tiles, axis=1)


def message_kernel(points_ref, labels_ref, scale_ref, krylov_ref, sources_ref, targets_ref, vector, row, copied, sem):
    taken = [
        pltpu.make_async_copy(krylov_ref.at[krylov_ref.shape[0] - 1], vector, sem.at[0]),
        pltpu.make_async_copy(points_ref, row.at[0:3], sem.at[1]),
        pltpu.make_async_copy(scale_ref, row.at[3:4], sem.at[2]),
        pltpu.make_async_copy(labels_ref, copied, sem.at[3]),
    ]
    for copy in taken:
        copy.start()
    for copy in taken:
        copy.wait()
    for k in range(sources_ref.shape[0]):
        sources_ref[k, 0:SYSTEMS, :] = vector[...]
        sources_ref[k, SYSTEMS : SYSTEMS + 4, :] = row[...]
    targets_ref[0, 0:3, :] = row[0:3, :]
    targets_ref[0, 3:4, :] = copied[...].astype(jnp.float32)


def messages(points, labels, shape_scale, krylov, count):
    hbm = pl.BlockSpec(memory_space=pltpu.HBM)
    return pl.pallas_call(
        message_kernel,
        out_shape=(
            jax.ShapeDtypeStruct((count, SYSTEMS + 4, LANES), jnp.float32),
            jax.ShapeDtypeStruct((1, 4, LANES), jnp.float32),
        ),
        in_specs=[hbm] * 4,
        out_specs=(VMEM,) * 2,
        scratch_shapes=[
            pltpu.VMEM((SYSTEMS, LANES), jnp.float32),
            pltpu.VMEM((4, LANES), jnp.float32),
            pltpu.VMEM((1, LANES), jnp.int32),
            pltpu.SemaphoreType.DMA((4,)),
        ],
        name="messages",
    )(points, labels[None, :], shape_scale[None, :], krylov)


def stored(rows, out_ref):
    zero = jnp.zeros(rows[0].shape, jnp.float32)
    for k, value in enumerate(rows + [zero] * (FEATS - len(rows))):
        out_ref[:, k, :] = value


def pair_of(ref, step):
    return wide([ref[2 * step], ref[2 * step + 1]])


def describe_sources(source_ref, feats_ref, weights_ref):
    coords = [source_ref[:, SYSTEMS + a, :] - 0.5 for a in range(3)]
    scale = source_ref[:, SYSTEMS + 3, :]
    per_square = 1.0 / (scale * scale)
    rows = []
    for value in [c * per_square for c in coords] + [per_square]:
        a, b, c = parts(value)
        rows += [a, a, b, b, a, c]
    square = coords[0] * coords[0] + coords[1] * coords[1] + coords[2] * coords[2]
    stored(rows + parts(square * per_square + 1.0), feats_ref)
    for step in range(weights_ref.shape[0]):
        weight = wide([source_ref[2 * step + j, 0:SYSTEMS, :] for j in range(2)])
        scale = wide([source_ref[2 * step + j, SYSTEMS + 3 : SYSTEMS + 4, :] for j in range(2)])
        terms = []
        for value in (weight / scale, weight * scale):
            first = value.astype(jnp.bfloat16)
            terms += [first, (value - first.astype(jnp.float32)).astype(jnp.bfloat16)]
        weights_ref[step] = jnp.concatenate(terms, axis=0)


def describe_targets(target_ref, feats_ref):
    coords = [target_ref[:, a, :] - 0.5 for a in range(3)]
    square = coords[0] * coords[0] + coords[1] * coords[1] + coords[2] * coords[2]
    rows = []
    for value in [-2.0 * c for c in coords] + [square]:
        a, b, c = parts(value)
        rows += [a, b, a, b, c, a]
    stored(rows + [jnp.ones(square.shape, jnp.float32)] * 3, feats_ref)


def products(sources, target_ref, target_feats, index):
    feats = pair_of(target_feats, index).astype(jnp.bfloat16)
    inner = wide([target_ref[2 * index + j, 3:4, :] for j in range(2)]) > 0.5
    total = jnp.zeros((4 * SYSTEMS, 2 * LANES), jnp.float32)
    for source_feats, weights in sources:
        for step in range(weights.shape[0]):
            ratio = lax.dot_general(
                pair_of(source_feats, step).astype(jnp.bfloat16),
                feats,
                (((0,), (0,)), ((), ())),
                preferred_element_type=jnp.float32,
            )
            root = lax.rsqrt(ratio)
            kernel = root * jnp.where(inner, 2.0 + root * root, ratio)
            first = kernel.astype(jnp.bfloat16)
            second = (kernel - first.astype(jnp.float32)).astype(jnp.bfloat16)
            weight = weights[step]
            total = (
                total
                + jnp.dot(weight, first, preferred_element_type=jnp.float32)
                + jnp.dot(weight, second, preferred_element_type=jnp.float32)
            )
    a, b, c, d = (total[k * SYSTEMS : (k + 1) * SYSTEMS] for k in range(4))
    result = jnp.where(inner, a + b, c + d)
    return result[:, :LANES], result[:, LANES:]


def near_kernel(*refs):
    (source_ref, target_ref, *before, out_ref, source_feats, weights, target_feats) = refs
    describe_sources(source_ref, source_feats, weights)
    describe_targets(target_ref, target_feats)
    for index in range(target_ref.shape[0] // 2):
        for j, part in enumerate(products([(source_feats, weights)], target_ref, target_feats, index)):
            out_ref[2 * index + j] = part + before[0][2 * index + j] if before else part


def far_kernel(first_feats, first_weights, second_feats, second_weights, target_ref, near_ref, out_ref, target_feats):
    describe_targets(target_ref, target_feats)
    place = lax.axis_index(COLUMN)
    near = near_ref.shape[0]
    for k in range(near):
        out_ref[jnp.bitwise_xor(place, k)] = near_ref[k]
    sources = [(first_feats, first_weights), (second_feats, second_weights)]
    for index in range(target_ref.shape[0] // 2):
        for j, part in enumerate(products(sources, target_ref, target_feats, index)):
            out_ref[jnp.bitwise_xor(place, near + 2 * index + j)] = part


def cost(sources, targets):
    pairs = sources * targets * LANES * LANES
    return pl.CostEstimate(flops=12 * SYSTEMS * pairs, bytes_accessed=2**20, transcendentals=pairs)


def near_product(sources, targets, *before):
    blocks, owners = sources.shape[0], targets.shape[0]
    return pl.pallas_call(
        near_kernel,
        out_shape=(
            jax.ShapeDtypeStruct((owners, SYSTEMS, LANES), jnp.float32),
            jax.ShapeDtypeStruct((blocks, FEATS, LANES), jnp.float32),
            jax.ShapeDtypeStruct((blocks // 2, 4 * SYSTEMS, 2 * LANES), jnp.bfloat16),
        ),
        in_specs=[VMEM] * (2 + len(before)),
        out_specs=(VMEM,) * 3,
        scratch_shapes=[pltpu.VMEM((owners, FEATS, LANES), jnp.float32)],
        cost_estimate=cost(blocks, owners),
        name="near",
        compiler_params=pltpu.CompilerParams(vmem_limit_bytes=16 * MIB),
    )(sources, targets, *before)


def far_product(described, targets, near):
    blocks, owners = sum(feats.shape[0] for feats in described[::2]), targets.shape[0]
    return pl.pallas_call(
        far_kernel,
        out_shape=jax.ShapeDtypeStruct((owners + near.shape[0], SYSTEMS, LANES), jnp.float32),
        in_specs=[VMEM] * (len(described) + 2),
        out_specs=VMEM,
        scratch_shapes=[pltpu.VMEM((owners, FEATS, LANES), jnp.float32)],
        cost_estimate=cost(blocks, owners),
        name="far",
        compiler_params=pltpu.CompilerParams(vmem_limit_bytes=16 * MIB),
    )(*described, targets, near)


def image_kernel(root, arrived_ref, sketch_ref, image_ref, local_ref):
    total = arrived_ref[0]
    for k in range(1, arrived_ref.shape[0]):
        total = total + arrived_ref[k]
    image = total / root
    image_ref[...] = image
    first = image.astype(jnp.bfloat16)
    second = (image - first.astype(jnp.float32)).astype(jnp.bfloat16)
    both = jnp.concatenate([first, second], axis=0)
    over_lanes = (((1,), (1,)), ((), ()))
    for k in range(sketch_ref.shape[0] // (2 * LANES)):
        rows = sketch_ref[2 * k * LANES : 2 * (k + 1) * LANES, :]
        high = rows.astype(jnp.bfloat16)
        low = (rows - high.astype(jnp.float32)).astype(jnp.bfloat16)
        total = lax.dot_general(both, high, over_lanes, preferred_element_type=jnp.float32)
        total = total + lax.dot_general(both, low, over_lanes, preferred_element_type=jnp.float32)
        total = total[:SYSTEMS] + total[SYSTEMS:]
        for j in range(2):
            local_ref[:, 2 * k + j, :] = total[:, j * LANES : (j + 1) * LANES]


def image_and_sketch(arrived, sketch, root):
    rows = sketch.shape[0]
    return pl.pallas_call(
        functools.partial(image_kernel, root),
        out_shape=(
            jax.ShapeDtypeStruct((SYSTEMS, LANES), jnp.float32),
            jax.ShapeDtypeStruct((SYSTEMS, rows // LANES, LANES), jnp.float32),
        ),
        in_specs=[VMEM] * 2,
        out_specs=(VMEM,) * 2,
        name="image",
        compiler_params=pltpu.CompilerParams(vmem_limit_bytes=8 * MIB),
    )(arrived, sketch)


def sum_kernel(arrived_ref, out_ref):
    total = arrived_ref[0]
    for k in range(1, arrived_ref.shape[0]):
        total = total + arrived_ref[k]
    for k in range(out_ref.shape[0]):
        out_ref[k] = total


def sum_for_each(arrived, count):
    return pl.pallas_call(
        sum_kernel,
        out_shape=jax.ShapeDtypeStruct((count, *arrived.shape[1:]), jnp.float32),
        in_specs=[VMEM],
        out_specs=VMEM,
        name="addup",
        compiler_params=pltpu.CompilerParams(vmem_limit_bytes=4 * MIB),
    )(arrived)


def project_kernel(arrived_ref, basis_ref, out_ref):
    sketched = arrived_ref[0]
    for k in range(1, arrived_ref.shape[0]):
        sketched = sketched + arrived_ref[k]
    lane = lax.broadcasted_iota(jnp.int32, (8, LANES), 1)

    def whole(value):
        return jnp.sum(jnp.sum(value, axis=1, keepdims=True), axis=0, keepdims=True)

    scalars = jnp.zeros((8, LANES), jnp.float32)
    remainder = sketched
    for j in range(KRYLOV):
        coefficient = whole(basis_ref[j] * sketched)
        scalars = jnp.where(lane == j, coefficient, scalars)
        remainder = remainder - coefficient * basis_ref[j]
    norm = jnp.sqrt(whole(remainder * remainder) / (sketched.shape[0] * LANES) + 1e-06)
    scalars = jnp.where(lane == KRYLOV, norm, scalars)
    message = jnp.concatenate([remainder / norm, scalars[0:1, :]], axis=0)
    for k in range(out_ref.shape[0]):
        for j in range(message.shape[0]):
            out_ref[k, :, j * LANES : (j + 1) * LANES] = message[j : j + 1, :]


def project(arrived, basis, count):
    return pl.pallas_call(
        project_kernel,
        out_shape=jax.ShapeDtypeStruct((count, 1, (arrived.shape[1] + 1) * LANES), jnp.float32),
        in_specs=[VMEM] * 2,
        out_specs=VMEM,
        name="project",
        compiler_params=pltpu.CompilerParams(vmem_limit_bytes=4 * MIB),
    )(arrived, basis)


def finish_kernel(arrived_ref, image_ref, krylov_ref, next_ref, coefficients_ref, sketch_ref, norms_ref):
    width = sketch_ref.shape[1]
    sketch_ref[...] = arrived_ref[:, 0, :width]
    scalars = arrived_ref[:, 0, width:]
    reduced = image_ref[...]
    for j in range(KRYLOV):
        reduced = reduced - scalars[:, j : j + 1] * krylov_ref[j]
    next_ref[...] = reduced / scalars[:, KRYLOV : KRYLOV + 1]
    across = jnp.transpose(scalars)
    coefficients_ref[...] = across[0:KRYLOV, :]
    norms_ref[...] = across[KRYLOV : KRYLOV + 1, :]


def finish(arrived, image, krylov):
    width = arrived.shape[2] - LANES
    return pl.pallas_call(
        finish_kernel,
        out_shape=(
            jax.ShapeDtypeStruct((SYSTEMS, LANES), jnp.float32),
            jax.ShapeDtypeStruct((KRYLOV, SYSTEMS), jnp.float32),
            jax.ShapeDtypeStruct((SYSTEMS, width), jnp.float32),
            jax.ShapeDtypeStruct((1, SYSTEMS), jnp.float32),
        ),
        in_specs=[VMEM] * 3,
        out_specs=(VMEM,) * 4,
        name="finish",
        compiler_params=pltpu.CompilerParams(vmem_limit_bytes=8 * MIB),
    )(arrived, image, krylov)


def step(points, labels, shape_scale, krylov_basis, sketch, sketched_basis):
    everything = lax.axis_size(ALL) * points.shape[1]
    system = lax.axis_index(OWNERS)
    basis = lax.dynamic_slice_in_dim(sketched_basis, system, 1, axis=1)
    basis = basis.reshape(KRYLOV, -1, LANES)
    sources, targets = messages(points, labels, shape_scale, krylov_basis, lax.axis_size(ROW))
    all_sources = exchange(sources, ROW)
    near = with_other(targets, COLUMN[2])
    near = with_other(near, COLUMN[1])
    far = swap(near, COLUMN[0])
    near, all_sources, basis = lax.optimization_barrier((near, all_sources, basis))
    other_sources = swap(all_sources, CORE)
    partial_value, *first = near_product(all_sources, near)
    partial_value, *second = near_product(other_sources, near, partial_value)
    partial_value = far_product((*first, *second), far, partial_value)
    image, local_sketch = image_and_sketch(
        exchange(partial_value, COLUMN), sketch, math.sqrt(everything)
    )
    over_owners = sum_for_each(exchange(local_sketch, OWNERS), lax.axis_size(LAYERS))
    message = project(exchange(over_owners, LAYERS), basis, lax.axis_size(OWNERS))
    next_vector, coefficients, sketch_next, norms = finish(
        exchange(message, OWNERS), image, krylov_basis
    )
    return (next_vector, coefficients, sketch_next, norms.reshape(-1))


def solution(mesh):
    torus = Mesh(mesh.devices.reshape((2,) * len(ALL)), ALL)
    in_specs = (P(None, ALL), P(ALL), P(ALL), P(None, None, ALL), P(None, ALL), P())
    out_specs = (P(None, ALL), P(), P(), P())
    return jax.shard_map(step, mesh=torus, in_specs=in_specs, out_specs=out_specs, check_vma=False)
```

time: 90 us -> 84.1 us (0.934)
  blocking collectives: 50.3 us -> 47.3 us
  starting transfers between devices: 20.9 us -> 19.8 us
    all_to_all x4, blocking collectives: 50.3 us -> 47.3 us  [exchange(): return lax.all_to_all(value, axis, 0, 0, tiled=True)]
    ppermute x4, waiting for transfers between devices: 2.22 us -> 1.02 us  [swap(): return lax.ppermute(value, axis, ((0, 1), (1, 0)))]
    ppermute x4, starting transfers between devices: 14.2 us -> 13.1 us  [swap(): return lax.ppermute(value, axis, ((0, 1), (1, 0)))]
    pallas_call x3 -> x4, Pallas kernels: 6.78 us -> 6.7 us  [the longest x2 3.7 us: near_product(): pl.pallas_call(near_kernel, out_shape=(jax.ShapeDtypeStruct((owners, SYST...]
  transfers between devices with their start and end apart: 5 -> 5, of which waited for: 3 -> 2; matrix products, arithmetic and copies ran while one was open for 0% -> 0% of each run, Pallas kernels for 4% -> 4%
where the time goes in v4:
time: 84.1 us; the launch traced here: 83.7 us
  blocking collectives  47.3 us (56%)
  starting transfers between devices  19.8 us (24%)
  Pallas kernels  9.72 us (12%)
  waiting for transfers between devices  5.36 us (6%)
    all_to_all x4, blocking collectives, exchange(): return lax.all_to_all(value, axis, 0, 0, tiled=True)  47.3 us
    ppermute x4, starting transfers between devices, swap(): return lax.ppermute(value, axis, ((0, 1), (1, 0)))  13.1 us
    all_to_all x1, starting transfers between devices, exchange(): return lax.all_to_all(value, axis, 0, 0, tiled=True)  6.75 us
    all_to_all x1, waiting for transfers between devices, exchange(): return lax.all_to_all(value, axis, 0, 0, tiled=True)  4.35 us
    pallas_call x2, Pallas kernels, near_product(): pl.pallas_call(near_kernel, out_shape=(jax.ShapeDtypeStruct((owners, SYST...  3.7 us
    pallas_call x1, Pallas kernels, far_product(): pl.pallas_call(far_kernel, out_shape=jax.ShapeDtypeStruct((owners + near....  2.74 us
  transfers between devices with their start and end apart: 5, of which 2 were waited for; matrix products, arithmetic and copies ran while one was open for 0% of the time, Pallas kernels for 4%

profile of v4, /device:TPU:1, one launch (start us, length us, event | category | flops | bytes accessed | tf_op | source)
XLA Modules:
  0.0 83.7 jit_solution(5734346712120117166)
XLA Ops:
  0.6 0.0 copy-start
  0.6 1.6 %messages.1 = (f32[16,36,128]{2,1,0:T(8,128)}, f32[1,4,128]{2,1,0:T(4,128)}) custom-call(f32[3,128]{1,0:T(4,128)} %points_ref.1, s32[1,128]{1,0:T(1,128)} %bitcast.5, f32[1,128]{1,0:T(1,128)} %bitcast.6, f32[8,32,128]{2,1,0:T(8,128)} %krylov_ref.3), custom_call_target="tpu_custom_call" | custom-call | tf_op jit(solution)/shard_map/messages/pallas_call | solution.py:68
  2.2 3.9 %collective-permute-start = (f32[1,4,128]{2,1,0:T(4,128)}, f32[1,4,128]{2,1,0:T(4,128)S(1)}, u32[]{:S(2)}, u32[]{:S(2)}) collective-permute-start(f32[1,4,128]{2,1,0:T(4,128)} %get-tuple-element.21), channel_id=1, source_target_pairs={{0,16},{16,0},{1,17},{17,1},{2,18},{18,2},{3,19},{19,3},{4,20},{20... | collective-permute-start | bytes 6152 | tf_op jit(solution)/shard_map/ppermute | solution.py:30
  6.1 6.8 %all-to-all-start = ((f32[16,36,128]{2,1,0:T(8,128)}), f32[16,36,128]{2,1,0:T(8,128)S(1)}, u32[]{:S(2)}, u32[]{:S(2)}) async-start(f32[16,36,128]{2,1,0:T(8,128)} %get-tuple-element.22), calls=%async_computation | async-start | bytes 655360 | tf_op jit(solution)/shard_map/all_to_all | solution.py:26
  12.9 0.0 copy-done
  12.9 0.0 copy-start.3
  13.0 0.6 copy-done.3
  13.6 0.0 collective-permute-done
  13.6 1.7 %collective-permute-start.1 = (f32[2,4,128]{2,1,0:T(4,128)S(1)}, f32[2,4,128]{2,1,0:T(4,128)S(1)}, u32[]{:S(2)}, u32[]{:S(2)}) collective-permute-start(f32[2,4,128]{2,1,0:T(4,128)S(1)} %pad_maximum_fusion), channel_id=1, source_target_pairs={{0,8},{8,0},{1,9},{9,1},{2,10},{10,2},{3,11},{11,3},{4,12},{12,4},... | collective-permute-start | bytes 12296 | tf_op jit(solution)/shard_map/ppermute | solution.py:30
  15.4 1.0 %collective-permute-done.1 = f32[2,4,128]{2,1,0:T(4,128)S(1)} collective-permute-done((f32[2,4,128]{2,1,0:T(4,128)S(1)}, f32[2,4,128]{2,1,0:T(4,128)S(1)}, u32[]{:S(2)}, u32[]{:S(2)}) %collective-permute-start.1) | collective-permute-done | bytes 4128 | tf_op jit(solution)/shard_map/ppermute | solution.py:30
  16.4 4.3 %all-to-all-done.refs_0_ = f32[16,36,128]{2,1,0:T(8,128)S(1)} async-done(((f32[16,36,128]{2,1,0:T(8,128)}), f32[16,36,128]{2,1,0:T(8,128)S(1)}, u32[]{:S(2)}, u32[]{:S(2)}) %all-to-all-start) | async-done | bytes 294944 | tf_op jit(solution)/shard_map/all_to_all | solution.py:26
  20.7 2.3 %collective-permute-start.2 = (f32[16,36,128]{2,1,0:T(8,128)S(1)}, f32[16,36,128]{2,1,0:T(8,128)S(1)}, u32[]{:S(2)}, u32[]{:S(2)}) collective-permute-start(f32[16,36,128]{2,1,0:T(8,128)S(1)} %all-to-all-done.refs_0_), channel_id=1, source_target_pairs={{0,1},{1,0},{2,3},{3,2},{4,5},{5,4},{6,7},{7,6},{8,9},{9,8},{10,11... | collective-permute-start | bytes 884744 | tf_op jit(solution)/shard_map/ppermute | solution.py:30
  23.0 5.1 %collective-permute-start.3 = (f32[4,4,128]{2,1,0:T(4,128)S(1)}, f32[4,4,128]{2,1,0:T(4,128)S(1)}, u32[]{:S(2)}, u32[]{:S(2)}) collective-permute-start(f32[4,4,128]{2,1,0:T(4,128)S(1)} %constant_dynamic-update-slice_fusion.refs_1_), channel_id=1, source_target_pairs={{0,32},{32,0},{1,33},{33,1},{2,34},{34,2},{3,35},{35,3},{4,36},{36... | collective-permute-start | bytes 24584 | tf_op jit(solution)/shard_map/ppermute | solution.py:30
  28.1 1.8 %near.2 = (f32[4,32,128]{2,1,0:T(8,128)S(1)}, f32[16,32,128]{2,1,0:T(8,128)S(1)}, bf16[8,128,256]{2,1,0:T(8,128)(2,1)S(1)}) custom-call(f32[16,36,128]{2,1,0:T(8,128)S(1)} %all-to-all-done.refs_0_, f32[4,4,128]{2,1,0:T(4,128)S(1)} %constant_dynamic-update-slice_fusion.refs_1_), custom_call_target="tpu_custom_call" | custom-call | flops 402653184 | bytes 1048576 | tf_op jit(solution)/shard_map/near/pallas_call | solution.py:181
  30.0 0.0 collective-permute-done.2.refs_0_
  30.0 1.9 %near.3 = (f32[4,32,128]{2,1,0:T(8,128)S(1)}, f32[16,32,128]{2,1,0:T(8,128)S(1)}, bf16[8,128,256]{2,1,0:T(8,128)(2,1)S(1)}) custom-call(f32[16,36,128]{2,1,0:T(8,128)S(1)} %collective-permute-done.2.refs_0_, f32[4,4,128]{2,1,0:T(4,128)S(1)} %constant_dynamic-update-slice_fusion.refs_1_, f32[4,32,128]{2,1,0:T(8,128)S(1)} %get-tuple-element.27.refs_2_), custom_call_target="tpu_custom_call" | custom-call | flops 402653184 | bytes 1048576 | tf_op jit(solution)/shard_map/near/pallas_call | solution.py:181
  31.9 0.0 collective-permute-done.3.target_ref
  31.9 0.0 copy-start.1
  31.9 2.7 %far.1 = f32[8,32,128]{2,1,0:T(8,128)S(1)} custom-call(f32[16,32,128]{2,1,0:T(8,128)S(1)} %get-tuple-element.25.first_feats, bf16[8,128,256]{2,1,0:T(8,128)(2,1)S(1)} %get-tuple-element.26.first_weights, f32[16,32,128]{2,1,0:T(8,128)S(1)} %get-tuple-element.28.second_feats, bf16[8,128,256]{2,1,0:T(8,128)(2,1)S(1)} %get-tuple-element.29.second_weights, ...), custom_call_target="tpu_custom_call" | custom-call | flops 805306368 | bytes 1048576 | tf_op jit(solution)/shard_map/far/pallas_call | solution.py:199
  34.6 11.8 %all_to_all.25.arrived_ref = f32[8,32,128]{2,1,0:T(8,128)S(1)} all-to-all(f32[8,32,128]{2,1,0:T(8,128)S(1)} %far.1), channel_id=1, replica_groups=mesh['x1'=2,'x0'=2,'z2'=2,'z1'=2,'z0'=2,'y1'=2,'y0'=2,'core'=2] {'z2','z..., dimensions={0} | all-to-all | bytes 262144 | tf_op jit(solution)/shard_map/all_to_all | solution.py:26
  46.4 0.0 copy-done.1
  46.4 0.3 image.1
  46.7 13.7 %all_to_all.26.arrived_ref = f32[32,8,128]{2,1,0:T(8,128)S(1)} all-to-all(f32[32,8,128]{2,1,0:T(8,128)S(1)} %get-tuple-element.31), channel_id=1, replica_groups=mesh['x1'=2,'x0'=2,'z2'=2,'z1'=2,'z0'=2,'y1'=2,'y0'=2,'core'=2] {'x1','x..., dimensions={0} | all-to-all | bytes 262144 | tf_op jit(solution)/shard_map/all_to_all | solution.py:26
  60.5 9.2 %all_to_all.27.arrived_ref = f32[8,8,128]{2,1,0:T(8,128)S(1)} all-to-all(f32[8,8,128]{2,1,0:T(8,128)S(1)} %addup.1), channel_id=1, replica_groups=mesh['x1'=2,'x0'=2,'z2'=2,'z1'=2,'z0'=2,'y1'=2,'y0'=2,'core'=2] {'z2','z..., dimensions={0} | all-to-all | bytes 65536 | tf_op jit(solution)/shard_map/all_to_all | solution.py:26
  69.7 0.3 project.1
  70.0 0.0 copy-start.2
  70.0 12.7 %all_to_all.28.arrived_ref = f32[32,1,1152]{2,1,0:T(1,128)S(1)} all-to-all(f32[32,1,1152]{2,1,0:T(1,128)S(1)} %project.1), channel_id=1, replica_groups=mesh['x1'=2,'x0'=2,'z2'=2,'z1'=2,'z0'=2,'y1'=2,'y0'=2,'core'=2] {'x1','x..., dimensions={0} | all-to-all | bytes 294912 | tf_op jit(solution)/shard_map/all_to_all | solution.py:26
  82.7 0.0 copy-done.2
  82.7 1.1 %finish.1 = (f32[32,128]{1,0:T(8,128)}, f32[8,32]{1,0:T(8,128)}, f32[32,1024]{1,0:T(8,128)}, f32[1,32]{1,0:T(1,128)}) custom-call(f32[32,1,1152]{2,1,0:T(1,128)S(1)} %all_to_all.28.arrived_ref, f32[32,128]{1,0:T(8,128)S(1)} %get-tuple-element.33.image_ref, f32[8,32,128]{2,1,0:T(8,128)S(1)} %copy-done.2), custom_call_target="tpu_custom_call" | custom-call | tf_op jit(solution)/shard_map/finish/pallas_call | solution.py:315
  (6 shorter events, 0.1 us)
Async XLA Ops:
  0.6 12.3 %copy-start = (f32[8,32,1024]{2,1,0:T(8,128)S(1)}, f32[8,32,1024]{2,1,0:T(8,128)}, u32[]{:S(2)}) copy-start(f32[8,32,1024]{2,1,0:T(8,128)} %param.11) | copy-start | bytes 3145732
  2.2 11.4 %collective-permute-start = (f32[1,4,128]{2,1,0:T(4,128)}, f32[1,4,128]{2,1,0:T(4,128)S(1)}, u32[]{:S(2)}, u32[]{:S(2)}) collective-permute-start(f32[1,4,128]{2,1,0:T(4,128)} %get-tuple-element.21), channel_id=1, source_target_pairs={{0,16},{16,0},{1,17},{17,1},{2,18},{18,2},{3,19},{19,3},{4,20},{20... | collective-permute-start | bytes 6152 | tf_op jit(solution)/shard_map/ppermute | solution.py:30
  6.1 14.6 %all-to-all-start = ((f32[16,36,128]{2,1,0:T(8,128)}), f32[16,36,128]{2,1,0:T(8,128)S(1)}, u32[]{:S(2)}, u32[]{:S(2)}) async-start(f32[16,36,128]{2,1,0:T(8,128)} %get-tuple-element.22), calls=%async_computation | async-start | bytes 655360 | tf_op jit(solution)/shard_map/all_to_all | solution.py:26
  12.9 0.7 copy-start.3
  13.6 2.7 %collective-permute-start.1 = (f32[2,4,128]{2,1,0:T(4,128)S(1)}, f32[2,4,128]{2,1,0:T(4,128)S(1)}, u32[]{:S(2)}, u32[]{:S(2)}) collective-permute-start(f32[2,4,128]{2,1,0:T(4,128)S(1)} %pad_maximum_fusion), channel_id=1, source_target_pairs={{0,8},{8,0},{1,9},{9,1},{2,10},{10,2},{3,11},{11,3},{4,12},{12,4},... | collective-permute-start | bytes 12296 | tf_op jit(solution)/shard_map/ppermute | solution.py:30
  20.7 9.3 %collective-permute-start.2 = (f32[16,36,128]{2,1,0:T(8,128)S(1)}, f32[16,36,128]{2,1,0:T(8,128)S(1)}, u32[]{:S(2)}, u32[]{:S(2)}) collective-permute-start(f32[16,36,128]{2,1,0:T(8,128)S(1)} %all-to-all-done.refs_0_), channel_id=1, source_target_pairs={{0,1},{1,0},{2,3},{3,2},{4,5},{5,4},{6,7},{7,6},{8,9},{9,8},{10,11... | collective-permute-start | bytes 884744 | tf_op jit(solution)/shard_map/ppermute | solution.py:30
  23.0 8.9 %collective-permute-start.3 = (f32[4,4,128]{2,1,0:T(4,128)S(1)}, f32[4,4,128]{2,1,0:T(4,128)S(1)}, u32[]{:S(2)}, u32[]{:S(2)}) collective-permute-start(f32[4,4,128]{2,1,0:T(4,128)S(1)} %constant_dynamic-update-slice_fusion.refs_1_), channel_id=1, source_target_pairs={{0,32},{32,0},{1,33},{33,1},{2,34},{34,2},{3,35},{35,3},{4,36},{36... | collective-permute-start | bytes 24584 | tf_op jit(solution)/shard_map/ppermute | solution.py:30
  31.9 14.5 %copy-start.1 = (f32[1024,128]{1,0:T(8,128)S(1)}, f32[1024,128]{1,0:T(8,128)}, u32[]{:S(2)}) copy-start(f32[1024,128]{1,0:T(8,128)} %sketch_ref.1) | copy-start | bytes 1572868
  70.0 12.7 %copy-start.2 = (f32[8,32,128]{2,1,0:T(8,128)S(1)}, f32[8,32,128]{2,1,0:T(8,128)}, u32[]{:S(2)}) copy-start(f32[8,32,128]{2,1,0:T(8,128)} %krylov_ref.3) | copy-start | bytes 393220

commit v5 on v4

--- a/solution.py
+++ b/solution.py
@@ -16,8 +16,8 @@
 X1, X0, Z2, Z1, Z0, Y1, Y0, CORE = ALL = ("x1", "x0", "z2", "z1", "z0", "y1", "y0", "core")
 COLUMN = (Z2, Z0, Z1)
 ROW = (X1, X0, Y1, Y0)
-OWNERS = (X1, X0, Y1, Y0, CORE)
-LAYERS = (Z2, Z1, Z0)
+OWNERS = (X1, X0, Y0, CORE)
+LAYERS = (Y1, Z2, Z1, Z0)
 VMEM = pl.BlockSpec(memory_space=pltpu.VMEM)
 MIB = 2**20
 
@@ -263,33 +263,40 @@
     )(arrived)
 
 
-def project_kernel(arrived_ref, basis_ref, out_ref):
-    sketched = arrived_ref[0]
+def project_kernel(share, arrived_ref, basis_ref, out_ref):
+    total = arrived_ref[0]
     for k in range(1, arrived_ref.shape[0]):
-        sketched = sketched + arrived_ref[k]
-    lane = lax.broadcasted_iota(jnp.int32, (8, LANES), 1)
+        total = total + arrived_ref[k]
+    rows = total.shape[0] // share
+    lane = lax.broadcasted_iota(jnp.int32, (1, LANES), 1)
 
     def whole(value):
         return jnp.sum(jnp.sum(value, axis=1, keepdims=True), axis=0, keepdims=True)
 
-    scalars = jnp.zeros((8, LANES), jnp.float32)
-    remainder = sketched
-    for j in range(KRYLOV):
-        coefficient = whole(basis_ref[j] * sketched)
-        scalars = jnp.where(lane == j, coefficient, scalars)
-        remainder = remainder - coefficient * basis_ref[j]
-    norm = jnp.sqrt(whole(remainder * remainder) / (sketched.shape[0] * LANES) + 1e-06)
-    scalars = jnp.where(lane == KRYLOV, norm, scalars)
-    message = jnp.concatenate([remainder / norm, scalars[0:1, :]], axis=0)
+    lines, last = [], []
+    for part in range(share):
+        sketched = total[part * rows : (part + 1) * rows]
+        basis = [basis_ref[j, part * rows : (part + 1) * rows, :] for j in range(KRYLOV)]
+        scalars = jnp.zeros((1, LANES), jnp.float32)
+        remainder = sketched
+        for j in range(KRYLOV):
+            coefficient = whole(basis[j] * sketched)
+            scalars = jnp.where(lane == j, coefficient, scalars)
+            remainder = remainder - coefficient * basis[j]
+        norm = jnp.sqrt(whole(remainder * remainder) / (rows * LANES) + 1e-06)
+        lines.append(remainder / norm)
+        last.append(jnp.where(lane == KRYLOV, norm, scalars))
+    message = jnp.concatenate(lines + last, axis=0)
     for k in range(out_ref.shape[0]):
         for j in range(message.shape[0]):
             out_ref[k, :, j * LANES : (j + 1) * LANES] = message[j : j + 1, :]
 
 
 def project(arrived, basis, count):
-    return pl.pallas_call(
-        project_kernel,
-        out_shape=jax.ShapeDtypeStruct((count, 1, (arrived.shape[1] + 1) * LANES), jnp.float32),
+    share = SYSTEMS // count
+    return pl.pallas_call(
+        functools.partial(project_kernel, share),
+        out_shape=jax.ShapeDtypeStruct((count, 1, (arrived.shape[1] + share) * LANES), jnp.float32),
         in_specs=[VMEM] * 2,
         out_specs=VMEM,
         name="project",
@@ -297,10 +304,19 @@
     )(arrived, basis)
 
 
-def finish_kernel(arrived_ref, image_ref, krylov_ref, next_ref, coefficients_ref, sketch_ref, norms_ref):
-    width = sketch_ref.shape[1]
-    sketch_ref[...] = arrived_ref[:, 0, :width]
-    scalars = arrived_ref[:, 0, width:]
+def finish_kernel(arrived_ref, image_ref, krylov_ref, next_ref, coefficients_ref, sketch_ref, norms_ref, lines):
+    width, count = sketch_ref.shape[1], arrived_ref.shape[0]
+    share = SYSTEMS // count
+    for part in range(share):
+        place = pl.ds(part, count, stride=share)
+        for k in range(width // LANES):
+            at = part * width + k * LANES
+            lines[k, place, :] = arrived_ref[:, 0, at : at + LANES]
+        at = share * width + part * LANES
+        lines[width // LANES, place, :] = arrived_ref[:, 0, at : at + LANES]
+    for k in range(width // LANES):
+        sketch_ref[:, k * LANES : (k + 1) * LANES] = lines[k]
+    scalars = lines[width // LANES]
     reduced = image_ref[...]
     for j in range(KRYLOV):
         reduced = reduced - scalars[:, j : j + 1] * krylov_ref[j]
@@ -311,7 +327,7 @@
 
 
 def finish(arrived, image, krylov):
-    width = arrived.shape[2] - LANES
+    width = arrived.shape[2] * arrived.shape[0] // SYSTEMS - LANES
     return pl.pallas_call(
         finish_kernel,
         out_shape=(
@@ -322,6 +338,7 @@
         ),
         in_specs=[VMEM] * 3,
         out_specs=(VMEM,) * 4,
+        scratch_shapes=[pltpu.VMEM((width // LANES + 1, SYSTEMS, LANES), jnp.float32)],
         name="finish",
         compiler_params=pltpu.CompilerParams(vmem_limit_bytes=8 * MIB),
     )(arrived, image, krylov)
@@ -330,7 +347,8 @@
 def step(points, labels, shape_scale, krylov_basis, sketch, sketched_basis):
     everything = lax.axis_size(ALL) * points.shape[1]
     system = lax.axis_index(OWNERS)
-    basis = lax.dynamic_slice_in_dim(sketched_basis, system, 1, axis=1)
+    share = SYSTEMS // lax.axis_size(OWNERS)
+    basis = lax.dynamic_slice_in_dim(sketched_basis, system * share, share, axis=1)
     basis = basis.reshape(KRYLOV, -1, LANES)
     sources, targets = messages(points, labels, shape_scale, krylov_basis, lax.axis_size(ROW))
     all_sources = exchange(sources, ROW)
@@ -345,6 +363,7 @@
     image, local_sketch = image_and_sketch(
         exchange(partial_value, COLUMN), sketch, math.sqrt(everything)
     )
+    local_sketch = local_sketch.reshape(lax.axis_size(OWNERS), -1, LANES)
     over_owners = sum_for_each(exchange(local_sketch, OWNERS), lax.axis_size(LAYERS))
     message = project(exchange(over_owners, LAYERS), basis, lax.axis_size(OWNERS))
     next_vector, coefficients, sketch_next, norms = finish(

time: 84.1 us -> 82 us (0.975)
  blocking collectives: 47.3 us -> 45.5 us
    all_to_all x4, blocking collectives: 47.3 us -> 45.5 us  [exchange(): return lax.all_to_all(value, axis, 0, 0, tiled=True)]
  transfers between devices with their start and end apart: 5 -> 5, of which waited for: 2 -> 2; matrix products, arithmetic and copies ran while one was open for 0% -> 0% of each run, Pallas kernels for 4% -> 5%
where the time goes in v5:
time: 82 us; the launch traced here: 81.6 us
  blocking collectives  45.5 us (55%)
  starting transfers between devices  19.8 us (24%)
  Pallas kernels  9.5 us (12%)
  waiting for transfers between devices  5.3 us (6%)
    all_to_all x4, blocking collectives, exchange(): return lax.all_to_all(value, axis, 0, 0, tiled=True)  45.5 us
    ppermute x4, starting transfers between devices, swap(): return lax.ppermute(value, axis, ((0, 1), (1, 0)))  13.1 us
    all_to_all x1, starting transfers between devices, exchange(): return lax.all_to_all(value, axis, 0, 0, tiled=True)  6.75 us
    all_to_all x1, waiting for transfers between devices, exchange(): return lax.all_to_all(value, axis, 0, 0, tiled=True)  4.28 us
    pallas_call x2, Pallas kernels, near_product(): pl.pallas_call(near_kernel, out_shape=(jax.ShapeDtypeStruct((owners, SYST...  3.71 us
    pallas_call x1, Pallas kernels, far_product(): pl.pallas_call(far_kernel, out_shape=jax.ShapeDtypeStruct((owners + near....  2.74 us
  transfers between devices with their start and end apart: 5, of which 2 were waited for; matrix products, arithmetic and copies ran while one was open for 0% of the time, Pallas kernels for 5%

profile of v5, /device:TPU:1, one launch (start us, length us, event | category | flops | bytes accessed | tf_op | source)
XLA Modules:
  0.0 81.6 jit_solution(9646718221640105046)
XLA Ops:
  0.6 0.0 copy-start
  0.6 1.6 %messages.1 = (f32[16,36,128]{2,1,0:T(8,128)}, f32[1,4,128]{2,1,0:T(4,128)}) custom-call(f32[3,128]{1,0:T(4,128)} %points_ref.1, s32[1,128]{1,0:T(1,128)} %bitcast.5, f32[1,128]{1,0:T(1,128)} %bitcast.6, f32[8,32,128]{2,1,0:T(8,128)} %krylov_ref.3), custom_call_target="tpu_custom_call" | custom-call | tf_op jit(solution)/shard_map/messages/pallas_call | solution.py:68
  2.2 3.9 %collective-permute-start = (f32[1,4,128]{2,1,0:T(4,128)}, f32[1,4,128]{2,1,0:T(4,128)S(1)}, u32[]{:S(2)}, u32[]{:S(2)}) collective-permute-start(f32[1,4,128]{2,1,0:T(4,128)} %get-tuple-element.21), channel_id=1, source_target_pairs={{0,16},{16,0},{1,17},{17,1},{2,18},{18,2},{3,19},{19,3},{4,20},{20... | collective-permute-start | bytes 6152 | tf_op jit(solution)/shard_map/ppermute | solution.py:30
  6.1 6.8 %all-to-all-start = ((f32[16,36,128]{2,1,0:T(8,128)}), f32[16,36,128]{2,1,0:T(8,128)S(1)}, u32[]{:S(2)}, u32[]{:S(2)}) async-start(f32[16,36,128]{2,1,0:T(8,128)} %get-tuple-element.22), calls=%async_computation | async-start | bytes 655360 | tf_op jit(solution)/shard_map/all_to_all | solution.py:26
  12.9 0.0 copy-done
  12.9 0.0 copy-start.3
  13.0 0.6 copy-done.3
  13.6 0.1 reshape.17.basis_ref
  13.7 0.0 collective-permute-done
  13.7 1.7 %collective-permute-start.1 = (f32[2,4,128]{2,1,0:T(4,128)S(1)}, f32[2,4,128]{2,1,0:T(4,128)S(1)}, u32[]{:S(2)}, u32[]{:S(2)}) collective-permute-start(f32[2,4,128]{2,1,0:T(4,128)S(1)} %pad_maximum_fusion), channel_id=1, source_target_pairs={{0,8},{8,0},{1,9},{9,1},{2,10},{10,2},{3,11},{11,3},{4,12},{12,4},... | collective-permute-start | bytes 12296 | tf_op jit(solution)/shard_map/ppermute | solution.py:30
  15.4 1.0 %collective-permute-done.1 = f32[2,4,128]{2,1,0:T(4,128)S(1)} collective-permute-done((f32[2,4,128]{2,1,0:T(4,128)S(1)}, f32[2,4,128]{2,1,0:T(4,128)S(1)}, u32[]{:S(2)}, u32[]{:S(2)}) %collective-permute-start.1) | collective-permute-done | bytes 4128 | tf_op jit(solution)/shard_map/ppermute | solution.py:30
  16.4 4.3 %all-to-all-done.refs_0_ = f32[16,36,128]{2,1,0:T(8,128)S(1)} async-done(((f32[16,36,128]{2,1,0:T(8,128)}), f32[16,36,128]{2,1,0:T(8,128)S(1)}, u32[]{:S(2)}, u32[]{:S(2)}) %all-to-all-start) | async-done | bytes 294944 | tf_op jit(solution)/shard_map/all_to_all | solution.py:26
  20.7 2.3 %collective-permute-start.2 = (f32[16,36,128]{2,1,0:T(8,128)S(1)}, f32[16,36,128]{2,1,0:T(8,128)S(1)}, u32[]{:S(2)}, u32[]{:S(2)}) collective-permute-start(f32[16,36,128]{2,1,0:T(8,128)S(1)} %all-to-all-done.refs_0_), channel_id=1, source_target_pairs={{0,1},{1,0},{2,3},{3,2},{4,5},{5,4},{6,7},{7,6},{8,9},{9,8},{10,11... | collective-permute-start | bytes 884744 | tf_op jit(solution)/shard_map/ppermute | solution.py:30
  23.0 5.1 %collective-permute-start.3 = (f32[4,4,128]{2,1,0:T(4,128)S(1)}, f32[4,4,128]{2,1,0:T(4,128)S(1)}, u32[]{:S(2)}, u32[]{:S(2)}) collective-permute-start(f32[4,4,128]{2,1,0:T(4,128)S(1)} %constant_dynamic-update-slice_fusion.refs_1_), channel_id=1, source_target_pairs={{0,32},{32,0},{1,33},{33,1},{2,34},{34,2},{3,35},{35,3},{4,36},{36... | collective-permute-start | bytes 24584 | tf_op jit(solution)/shard_map/ppermute | solution.py:30
  28.1 1.8 %near.2 = (f32[4,32,128]{2,1,0:T(8,128)S(1)}, f32[16,32,128]{2,1,0:T(8,128)S(1)}, bf16[8,128,256]{2,1,0:T(8,128)(2,1)S(1)}) custom-call(f32[16,36,128]{2,1,0:T(8,128)S(1)} %all-to-all-done.refs_0_, f32[4,4,128]{2,1,0:T(4,128)S(1)} %constant_dynamic-update-slice_fusion.refs_1_), custom_call_target="tpu_custom_call" | custom-call | flops 402653184 | bytes 1048576 | tf_op jit(solution)/shard_map/near/pallas_call | solution.py:181
  30.0 0.0 collective-permute-done.2.refs_0_
  30.0 1.9 %near.3 = (f32[4,32,128]{2,1,0:T(8,128)S(1)}, f32[16,32,128]{2,1,0:T(8,128)S(1)}, bf16[8,128,256]{2,1,0:T(8,128)(2,1)S(1)}) custom-call(f32[16,36,128]{2,1,0:T(8,128)S(1)} %collective-permute-done.2.refs_0_, f32[4,4,128]{2,1,0:T(4,128)S(1)} %constant_dynamic-update-slice_fusion.refs_1_, f32[4,32,128]{2,1,0:T(8,128)S(1)} %get-tuple-element.27.refs_2_), custom_call_target="tpu_custom_call" | custom-call | flops 402653184 | bytes 1048576 | tf_op jit(solution)/shard_map/near/pallas_call | solution.py:181
  31.9 0.0 collective-permute-done.3.target_ref
  31.9 0.0 copy-start.1
  31.9 2.7 %far.1 = f32[8,32,128]{2,1,0:T(8,128)S(1)} custom-call(f32[16,32,128]{2,1,0:T(8,128)S(1)} %get-tuple-element.25.first_feats, bf16[8,128,256]{2,1,0:T(8,128)(2,1)S(1)} %get-tuple-element.26.first_weights, f32[16,32,128]{2,1,0:T(8,128)S(1)} %get-tuple-element.28.second_feats, bf16[8,128,256]{2,1,0:T(8,128)(2,1)S(1)} %get-tuple-element.29.second_weights, ...), custom_call_target="tpu_custom_call" | custom-call | flops 805306368 | bytes 1048576 | tf_op jit(solution)/shard_map/far/pallas_call | solution.py:199
  34.7 11.8 %all_to_all.25.arrived_ref = f32[8,32,128]{2,1,0:T(8,128)S(1)} all-to-all(f32[8,32,128]{2,1,0:T(8,128)S(1)} %far.1), channel_id=1, replica_groups=mesh['x1'=2,'x0'=2,'z2'=2,'z1'=2,'z0'=2,'y1'=2,'y0'=2,'core'=2] {'z2','z..., dimensions={0} | all-to-all | bytes 262144 | tf_op jit(solution)/shard_map/all_to_all | solution.py:26
  46.4 0.0 copy-done.1
  46.4 0.3 image.1
  46.8 11.1 %all_to_all.26.arrived_ref = f32[16,16,128]{2,1,0:T(8,128)S(1)} all-to-all(f32[16,16,128]{2,1,0:T(8,128)S(1)} %bitcast.4), channel_id=1, replica_groups=mesh['x1'=2,'x0'=2,'z2'=2,'z1'=2,'z0'=2,'y1'=2,'y0'=2,'core'=2] {'x1','x..., dimensions={0} | all-to-all | bytes 262144 | tf_op jit(solution)/shard_map/all_to_all | solution.py:26
  57.9 11.7 %all_to_all.27.arrived_ref = f32[16,16,128]{2,1,0:T(8,128)S(1)} all-to-all(f32[16,16,128]{2,1,0:T(8,128)S(1)} %addup.1), channel_id=1, replica_groups=mesh['x1'=2,'x0'=2,'z2'=2,'z1'=2,'z0'=2,'y1'=2,'y0'=2,'core'=2] {'y1','z..., dimensions={0} | all-to-all | bytes 262144 | tf_op jit(solution)/shard_map/all_to_all | solution.py:26
  69.5 0.3 project.1
  69.8 0.0 copy-start.2
  69.8 11.0 %all_to_all.28.arrived_ref = f32[16,1,2304]{2,1,0:T(1,128)S(1)} all-to-all(f32[16,1,2304]{2,1,0:T(1,128)S(1)} %project.1), channel_id=1, replica_groups=mesh['x1'=2,'x0'=2,'z2'=2,'z1'=2,'z0'=2,'y1'=2,'y0'=2,'core'=2] {'x1','x..., dimensions={0} | all-to-all | bytes 294912 | tf_op jit(solution)/shard_map/all_to_all | solution.py:26
  80.8 0.0 copy-done.2
  80.8 0.8 finish.1
  (6 shorter events, 0.1 us)
Async XLA Ops:
  0.6 12.3 %copy-start = (f32[8,32,1024]{2,1,0:T(8,128)S(1)}, f32[8,32,1024]{2,1,0:T(8,128)}, u32[]{:S(2)}) copy-start(f32[8,32,1024]{2,1,0:T(8,128)} %param.11) | copy-start | bytes 3145732
  2.2 11.4 %collective-permute-start = (f32[1,4,128]{2,1,0:T(4,128)}, f32[1,4,128]{2,1,0:T(4,128)S(1)}, u32[]{:S(2)}, u32[]{:S(2)}) collective-permute-start(f32[1,4,128]{2,1,0:T(4,128)} %get-tuple-element.21), channel_id=1, source_target_pairs={{0,16},{16,0},{1,17},{17,1},{2,18},{18,2},{3,19},{19,3},{4,20},{20... | collective-permute-start | bytes 6152 | tf_op jit(solution)/shard_map/ppermute | solution.py:30
  6.1 14.6 %all-to-all-start = ((f32[16,36,128]{2,1,0:T(8,128)}), f32[16,36,128]{2,1,0:T(8,128)S(1)}, u32[]{:S(2)}, u32[]{:S(2)}) async-start(f32[16,36,128]{2,1,0:T(8,128)} %get-tuple-element.22), calls=%async_computation | async-start | bytes 655360 | tf_op jit(solution)/shard_map/all_to_all | solution.py:26
  12.9 0.7 copy-start.3
  13.7 2.7 %collective-permute-start.1 = (f32[2,4,128]{2,1,0:T(4,128)S(1)}, f32[2,4,128]{2,1,0:T(4,128)S(1)}, u32[]{:S(2)}, u32[]{:S(2)}) collective-permute-start(f32[2,4,128]{2,1,0:T(4,128)S(1)} %pad_maximum_fusion), channel_id=1, source_target_pairs={{0,8},{8,0},{1,9},{9,1},{2,10},{10,2},{3,11},{11,3},{4,12},{12,4},... | collective-permute-start | bytes 12296 | tf_op jit(solution)/shard_map/ppermute | solution.py:30
  20.7 9.3 %collective-permute-start.2 = (f32[16,36,128]{2,1,0:T(8,128)S(1)}, f32[16,36,128]{2,1,0:T(8,128)S(1)}, u32[]{:S(2)}, u32[]{:S(2)}) collective-permute-start(f32[16,36,128]{2,1,0:T(8,128)S(1)} %all-to-all-done.refs_0_), channel_id=1, source_target_pairs={{0,1},{1,0},{2,3},{3,2},{4,5},{5,4},{6,7},{7,6},{8,9},{9,8},{10,11... | collective-permute-start | bytes 884744 | tf_op jit(solution)/shard_map/ppermute | solution.py:30
  23.0 8.9 %collective-permute-start.3 = (f32[4,4,128]{2,1,0:T(4,128)S(1)}, f32[4,4,128]{2,1,0:T(4,128)S(1)}, u32[]{:S(2)}, u32[]{:S(2)}) collective-permute-start(f32[4,4,128]{2,1,0:T(4,128)S(1)} %constant_dynamic-update-slice_fusion.refs_1_), channel_id=1, source_target_pairs={{0,32},{32,0},{1,33},{33,1},{2,34},{34,2},{3,35},{35,3},{4,36},{36... | collective-permute-start | bytes 24584 | tf_op jit(solution)/shard_map/ppermute | solution.py:30
  31.9 14.5 %copy-start.1 = (f32[1024,128]{1,0:T(8,128)S(1)}, f32[1024,128]{1,0:T(8,128)}, u32[]{:S(2)}) copy-start(f32[1024,128]{1,0:T(8,128)} %sketch_ref.1) | copy-start | bytes 1572868
  69.8 11.0 %copy-start.2 = (f32[8,32,128]{2,1,0:T(8,128)S(1)}, f32[8,32,128]{2,1,0:T(8,128)}, u32[]{:S(2)}) copy-start(f32[8,32,128]{2,1,0:T(8,128)} %krylov_ref.3) | copy-start | bytes 393220
